TPU v7x, 8 devices: a whole 2x2x1 slice. The times are simulated.
8 devices in a mesh: dp: 1 (over z), ws: 8 (over y, x, core).
Axes of the slice: x: 2, y: 2, z: 1, core: 2. Of those that a mesh axis runs over, the one named last changes fastest.
Arguments:
- hidden: bfloat16 [128, 768], P(('dp', 'ws'))
- self_k: bfloat16 [128, 12, 512, 64], P(('dp', 'ws'))
- self_v: bfloat16 [128, 12, 512, 64], P(('dp', 'ws'))
- cross_k: bfloat16 [128, 12, 384, 64], P(('dp', 'ws'))
- cross_v: bfloat16 [128, 12, 384, 64], P(('dp', 'ws'))
- positions: int32 [128], P(('dp', 'ws'))
- enc_mask: int32 [128, 384], P(('dp', 'ws'))
- rel_bias: float32 [12, 512], replicated
- expert_idx: int32 [128], P(('dp', 'ws'))
- ln_self: float32 [768], replicated
- ln_cross: float32 [768], replicated
- ln_ffn: float32 [768], replicated
- wq_self: bfloat16 [768, 768], P(None, 'ws')
- wk_self: bfloat16 [768, 768], P(None, 'ws')
- wv_self: bfloat16 [768, 768], P(None, 'ws')
- wo_self: bfloat16 [768, 768], P(None, 'ws')
- wq_cross: bfloat16 [768, 768], P(None, 'ws')
- wo_cross: bfloat16 [768, 768], P(None, 'ws')
- w_router: float32 [768, 8], P(None, 'ws')
- w_in: bfloat16 [8, 768, 3072], P(None, None, 'ws')
- w_out: bfloat16 [8, 3072, 768], P(None, 'ws')
Outputs:
- output 1: bfloat16 [128, 768], P(('dp', 'ws'))
- output 2: bfloat16 [128, 12, 512, 64], P(('dp', 'ws'))
- output 3: bfloat16 [128, 12, 512, 64], P(('dp', 'ws'))
All inputs are finite; a program needn't handle non-finite values.
Results may differ from a plain program's by a relative error of at most 0.0114859.
Values are sent between devices in bfloat16 or wider.
A program may use at most 1 GiB of HBM per device.

v0:
```python
import functools
import jax
import jax.numpy as jnp
from jax import lax
from jax.sharding import PartitionSpec as P

EPSILON = 1e-6
NEG_BIG = -1e30


def rms_norm(hidden, scale):
    hid_f32 = hidden.astype(jnp.float32)
    inv_rms = lax.rsqrt(jnp.mean(hid_f32 * hid_f32, axis=-1, keepdims=True) + EPSILON)
    return (hid_f32 * inv_rms * scale).astype(jnp.bfloat16)


def project(x_norm, weight):
    return jnp.dot(x_norm, weight, preferred_element_type=jnp.float32).astype(jnp.bfloat16)


def attend(queries, cache_keys, cache_vals, score_bias):
    scores = jnp.einsum('bhd,bhld->bhl', queries, cache_keys, preferred_element_type=jnp.float32) + score_bias
    attn_probs = jax.nn.softmax(scores, axis=-1).astype(jnp.bfloat16)
    context = jnp.einsum('bhl,bhld->bhd', attn_probs, cache_vals, preferred_element_type=jnp.float32)
    return context.astype(jnp.bfloat16)


def self_bias(rel_bias, positions, cache_len):
    distance = positions[:, None] - jnp.arange(cache_len)[None, :]
    pos_bias = jnp.take(rel_bias, jnp.clip(distance, 0, cache_len - 1), axis=1)
    pos_bias = jnp.where(distance[None] >= 0, pos_bias, NEG_BIG).transpose(1, 0, 2)
    return distance, pos_bias


def solution(mesh):
    ws_size = mesh.shape['ws']
    row_axes = ('dp', 'ws')
    row_vec = P(row_axes)
    row_mat = P(row_axes, None)
    cache_spec = P(row_axes, None, None, None)
    col_split = P(None, 'ws')
    in_specs = (row_mat, cache_spec, cache_spec, cache_spec, cache_spec, row_vec, row_mat, P(None, None), row_vec,
                P(None), P(None), P(None), col_split, col_split, col_split, col_split, col_split, col_split,
                col_split, P(None, None, 'ws'), P(None, 'ws', None))
    out_specs = (row_mat, cache_spec, cache_spec)

    def decoder_block(hidden, self_k, self_v, cross_k, cross_v, positions, enc_mask, rel_bias, expert_idx,
                      ln_self, ln_cross, ln_ffn, wq_self, wk_self, wv_self, wo_self, wq_cross, wo_cross,
                      w_router, w_in, w_out):
        gather_ws = functools.partial(lax.all_gather, axis_name='ws', tiled=True)
        wq_full = gather_ws(wq_self, axis=1)
        wk_full = gather_ws(wk_self, axis=1)
        wv_full = gather_ws(wv_self, axis=1)
        wo_full = gather_ws(wo_self, axis=1)
        wqc_full = gather_ws(wq_cross, axis=1)
        woc_full = gather_ws(wo_cross, axis=1)
        router_full = gather_ws(w_router, axis=1)
        win_full = gather_ws(w_in, axis=2)
        wout_full = gather_ws(w_out, axis=1)
        idx_all = gather_ws(expert_idx, axis=0)

        local_rows = hidden.shape[0]
        num_heads = rel_bias.shape[0]
        head_shape = (local_rows, num_heads, wq_full.shape[1] // num_heads)
        experts = win_full.shape[0]
        group_rows = local_rows * ws_size
        capacity = (2 * group_rows + experts - 1) // experts

        x_norm = rms_norm(hidden, ln_self)
        queries = project(x_norm, wq_full).reshape(head_shape)
        k_new = project(x_norm, wk_full).reshape(head_shape)
        v_new = project(x_norm, wv_full).reshape(head_shape)
        distance, pos_bias = self_bias(rel_bias, positions, self_k.shape[2])
        write_mask = (distance == 0)[:, None, :, None]
        new_self_k = jnp.where(write_mask, k_new[:, :, None, :], self_k)
        new_self_v = jnp.where(write_mask, v_new[:, :, None, :], self_v)
        context = attend(queries, new_self_k, new_self_v, pos_bias).reshape(local_rows, -1)
        after_self = (hidden.astype(jnp.float32) + jnp.dot(context, wo_full, preferred_element_type=jnp.float32)).astype(jnp.bfloat16)

        x_norm = rms_norm(after_self, ln_cross)
        queries = project(x_norm, wqc_full).reshape(head_shape)
        mask_bias = jnp.where(enc_mask == 1, 0.0, NEG_BIG)[:, None, :]
        context = attend(queries, cross_k, cross_v, mask_bias).reshape(local_rows, -1)
        after_cross = (after_self.astype(jnp.float32) + jnp.dot(context, woc_full, preferred_element_type=jnp.float32)).astype(jnp.bfloat16)

        x_norm = rms_norm(after_cross, ln_ffn)
        logits = jnp.dot(x_norm.astype(jnp.float32), router_full, precision=lax.Precision.HIGHEST,
                         preferred_element_type=jnp.float32)
        router_probs = jax.nn.softmax(logits, axis=-1)
        chosen = jnp.arange(experts)[None, :] == expert_idx[:, None]
        gate_val = jnp.sum(jnp.where(chosen, router_probs, 0.0), axis=-1)
        row_ids = lax.axis_index('ws') * local_rows + jnp.arange(local_rows)
        earlier = (idx_all[None, :] == expert_idx[:, None]) & (jnp.arange(group_rows)[None, :] < row_ids[:, None])
        slot_idx = jnp.sum(earlier.astype(jnp.int32), axis=1)
        keep_gate = jnp.where(slot_idx < capacity, gate_val, 0.0)
        ffn_hidden = jnp.einsum('bd,bdf->bf', x_norm, jnp.take(win_full, expert_idx, axis=0),
                                preferred_element_type=jnp.float32)
        ffn_hidden = jax.nn.relu(ffn_hidden).astype(jnp.bfloat16)
        expert_out = jnp.einsum('bf,bfd->bd', ffn_hidden, jnp.take(wout_full, expert_idx, axis=0),
                                preferred_element_type=jnp.float32).astype(jnp.bfloat16)
        hidden_out = (after_cross.astype(jnp.float32) + expert_out.astype(jnp.float32) * keep_gate[:, None]).astype(jnp.bfloat16)
        return hidden_out, new_self_k, new_self_v

    return jax.shard_map(decoder_block, mesh=mesh, in_specs=in_specs, out_specs=out_specs, check_vma=False)
```

profile of v0, /device:TPU:0, one launch (start us, length us, event | category | flops | bytes accessed | tf_op | source)
XLA Modules:
  0.0 592.3 jit_solution(2408232517432982015)
XLA Ops:
  7.2 0.0 all-gather.12.cloned.1.call-start
  7.3 0.7 all-gather.12.cloned.1.call-update
  8.0 0.0 all-gather.14.cloned.1.call-start
  8.0 0.7 all-gather.14.cloned.1.call-update
  8.7 0.0 all-gather.10.cloned.1.call-start
  8.8 0.7 all-gather.10.cloned.1.call-update
  9.4 0.0 all-gather.16.cloned.1.call-start
  9.5 0.5 all-gather.16.cloned.1.call-update
  10.0 0.0 all-gather.18.cloned.1.call-start
  10.1 0.5 all-gather.18.cloned.1.call-update
  10.6 0.0 all-gather.20.cloned.1.call-start
  10.7 0.5 all-gather.20.cloned.1.call-update
  11.2 0.0 all-gather.22.cloned.1.call-start
  11.2 0.7 all-gather.22.cloned.1.call-update
  11.9 0.0 all-gather.24.cloned.1.call-start
  12.0 0.7 all-gather.24.cloned.1.call-update
  12.7 0.9 copy.27
  13.6 0.7 fusion.40
  14.4 27.7 %gather_fusion = f32[8192,12]{1,0:T(8,128)} fusion(f32[12,512]{0,1:T(8,128)S(1)} %copy.27, s32[8192]{0:T(1024)S(1)} %broadcast_clamp_fusion), kind=kCustom, calls=%fused_computation | custom fusion | bytes 819200 | tf_op jit(solution)/shard_map/jit(_take)/gather | solution.py:30
  42.1 0.2 dynamic-update-slice
  42.3 25.0 %all-reduce = s32[128]{0:T(128)S(1)} all-reduce(s32[128]{0:T(128)S(1)} %dynamic-update-slice), channel_id=1, replica_groups=mesh['dp'=1,'ws'=8] {'ws'}, use_global_device_ids=true, to_apply=%add | all-reduce | flops 128 | bytes 1024
  67.3 11.8 %all-gather = f32[8,1,768]{2,1,0:T(1,128)S(1)} all-gather(f32[1,1,768]{2,1,0:T(1,128)S(1)} %bitcast.75), channel_id=1, replica_groups=mesh['dp'=1,'ws'=8] {'ws'}, dimensions={0}, use_global_device_ids=true | all-gather | bytes 27648 | tf_op jit(solution)/shard_map/all_gather | solution.py:57
  79.2 0.1 fusion.36
  79.3 0.2 convert_reduce_fusion
  79.5 0.1 fusion.45
  79.6 0.0 all-gather.12.cloned.1.call-done
  79.7 1.7 convolution_convert_fusion.2
  81.4 0.1 broadcast_in_dim.113
  81.5 1.7 convolution_convert_fusion.1
  83.3 0.1 broadcast_in_dim.119
  83.4 1.7 convolution_convert_fusion.3
  85.1 0.1 reshape.253
  85.3 14.4 %broadcast_select_fusion = (bf16[16,12,512,64]{2,3,1,0:T(8,128)(2,1)}, bf16[16,12,512,64]{2,3,1,0:T(8,128)(2,1)S(1)}) fusion(bf16[16,12,512,64]{2,3,1,0:T(8,128)(2,1)} %param.23, pred[16,512]{1,0:T(8,128)(4,1)S(1)} %get-tuple-element.13, bf16[16,12,64]{2,1,0:T(8,128)(2,1)S(1)} %broadcast_in_dim.119, bf16[16,12,512,64]{2,3,1,0:T(8,128)(2,1)} %param.22, ...), kind=kLoop, calls=%fused_computation.27 | loop fusion | flops 12582912 | bytes 50388992 | tf_op jit(solution)/shard_map/jit(_where)/select_n | solution.py:76
  99.7 4.8 copy-done
  104.5 1.7 fusion.71
  106.2 3.4 copy.29
  109.5 5.6 fusion.18
  115.2 2.6 copy.30
  117.8 6.4 %fusion.72 = bf16[16,12,1,64]{3,2,1,0:T(2,128)(2,1)S(1)} fusion(bf16[16,12,512,1]{2,3,1,0:T(2,128)(2,1)S(1)} %copy.30, bf16[16,12,512,64]{2,3,1,0:T(8,128)(2,1)} %get-tuple-element.9), kind=kOutput, calls=%fused_computation.117 | convolution fusion | flops 12582912 | bytes 12804096 | tf_op jit(solution)/shard_map/bhl,bhld->bhd/dot_general | solution.py:24
  124.2 0.1 reshape.168
  124.3 1.8 multiply_reduce_fusion.1
  126.2 1.7 convolution_convert_fusion
  127.9 0.1 reshape.255
  128.1 5.4 fusion.73
  133.5 0.2 fusion.24
  133.7 7.0 %fusion.29 = bf16[16,12,1,64]{3,2,1,0:T(2,128)(2,1)S(1)} fusion(bf16[16,12,384,64]{2,3,1,0:T(8,128)(2,1)} %param.25, bf16[16,12,384,1]{2,0,1,3:T(8,128)(2,1)S(1)} %fusion.24), kind=kOutput, calls=%fused_computation.50 | convolution fusion | flops 9437184 | bytes 9609216 | tf_op jit(solution)/shard_map/bhl,bhld->bhd/dot_general | solution.py:24
  140.8 0.1 reshape.170
  140.9 1.8 multiply_reduce_fusion
  142.8 0.2 fusion.70
  143.1 0.5 compare_select_fusion.4
  143.6 0.1 fusion.64
  143.7 170.3 %all-gather.22.cloned.1.call-done = bf16[8,768,3072]{2,1,0:T(8,128)(2,1)} async-done(((bf16[8,768,384]{2,1,0:T(8,128)(2,1)}), bf16[8,768,3072]{2,1,0:T(8,128)(2,1)}) %all-gather.22.cloned.1.call-update) | async-done | bytes 37748752 | tf_op jit(solution)/shard_map/all_gather | solution.py:58
  314.0 24.4 %fusion.68 = (bf16[8,768,1024]{2,1,0:T(8,128)(2,1)}, bf16[8,768,1024]{2,1,0:T(8,128)(2,1)}, bf16[8,768,1024]{2,1,0:T(8,128)(2,1)}) fusion(bf16[8,768,3072]{2,1,0:T(8,128)(2,1)} %all-gather.22.cloned.1.call-done), kind=kLoop, calls=%fused_computation.113 | loop fusion | bytes 75497472 | tf_op jit(solution)/shard_map/jit(_take)/gather | solution.py:96
  338.4 14.6 %gather_fusion.1 = bf16[16,768,1024]{2,1,0:T(8,128)(2,1)} fusion(bf16[8,768,1024]{2,1,0:T(8,128)(2,1)} %get-tuple-element.3, s32[1024]{0:T(1024)S(1)} %pad_clamp_fusion), kind=kCustom, calls=%fused_computation.1 | custom fusion | bytes 50331712 | tf_op jit(solution)/shard_map/jit(_take)/gather | solution.py:96
  353.0 14.7 %gather_fusion.2 = bf16[16,768,1024]{2,1,0:T(8,128)(2,1)} fusion(bf16[8,768,1024]{2,1,0:T(8,128)(2,1)} %get-tuple-element.4, s32[1024]{0:T(1024)S(1)} %pad_clamp_fusion), kind=kCustom, calls=%fused_computation.2 | custom fusion | bytes 50331712 | tf_op jit(solution)/shard_map/jit(_take)/gather | solution.py:96
  367.7 14.9 %gather_fusion.3 = bf16[16,768,1024]{2,1,0:T(8,128)(2,1)} fusion(bf16[8,768,1024]{2,1,0:T(8,128)(2,1)} %get-tuple-element.5, s32[1024]{0:T(1024)S(1)} %pad_clamp_fusion), kind=kCustom, calls=%fused_computation.3 | custom fusion | bytes 50331712 | tf_op jit(solution)/shard_map/jit(_take)/gather | solution.py:96
  382.6 27.4 %fusion.4 = bf16[16,1,3072]{2,1,0:T(2,128)(2,1)S(1)} fusion(bf16[16,768,1024]{2,1,0:T(8,128)(2,1)} %gather_fusion.3, bf16[16,768,1024]{2,1,0:T(8,128)(2,1)} %gather_fusion.2, bf16[16,768,1024]{2,1,0:T(8,128)(2,1)} %gather_fusion.1, pred[16]{0:T(512)(128)(4,1)S(1)} %compare_and_fusion, bf16[16,768,1]{1,0,2:T(8,128)(2,1)S(1)} %fusion.64), kind=kOutput, calls=%fused_computation.12 | convolution fusion | flops 339738624 | bytes 75620368 | tf_op jit(solution)/shard_map/bd,bdf->bf/dot_general | solution.py:96
  410.1 79.7 %all-gather.24.cloned.1.call-done = bf16[8,3072,768]{2,1,0:T(8,128)(2,1)} async-done(((bf16[8,384,768]{2,1,0:T(8,128)(2,1)}), bf16[8,3072,768]{2,1,0:T(8,128)(2,1)}) %all-gather.24.cloned.1.call-update) | async-done | bytes 37748752 | tf_op jit(solution)/shard_map/all_gather | solution.py:59
  489.8 25.3 %fusion.69 = (bf16[8,1024,768]{2,1,0:T(8,128)(2,1)}, bf16[8,1024,768]{2,1,0:T(8,128)(2,1)}, bf16[8,1024,768]{2,1,0:T(8,128)(2,1)}) fusion(bf16[8,3072,768]{2,1,0:T(8,128)(2,1)} %all-gather.24.cloned.1.call-done), kind=kLoop, calls=%fused_computation.114 | loop fusion | bytes 75497472 | tf_op jit(solution)/shard_map/jit(_take)/gather | solution.py:99
  515.2 14.7 %gather_fusion.4 = bf16[16,1024,768]{2,1,0:T(8,128)(2,1)} fusion(bf16[8,1024,768]{2,1,0:T(8,128)(2,1)} %get-tuple-element.6, s32[1024]{0:T(1024)S(1)} %pad_clamp_fusion), kind=kCustom, calls=%fused_computation.4 | custom fusion | bytes 50331712 | tf_op jit(solution)/shard_map/jit(_take)/gather | solution.py:99
  529.8 14.7 %gather_fusion.5 = bf16[16,1024,768]{2,1,0:T(8,128)(2,1)} fusion(bf16[8,1024,768]{2,1,0:T(8,128)(2,1)} %get-tuple-element.7, s32[1024]{0:T(1024)S(1)} %pad_clamp_fusion), kind=kCustom, calls=%fused_computation.5 | custom fusion | bytes 50331712 | tf_op jit(solution)/shard_map/jit(_take)/gather | solution.py:99
  544.5 14.7 %gather_fusion.6 = bf16[16,1024,768]{2,1,0:T(8,128)(2,1)} fusion(bf16[8,1024,768]{2,1,0:T(8,128)(2,1)} %get-tuple-element.8, s32[1024]{0:T(1024)S(1)} %pad_clamp_fusion), kind=kCustom, calls=%fused_computation.6 | custom fusion | bytes 50331712 | tf_op jit(solution)/shard_map/jit(_take)/gather | solution.py:99
  559.2 25.6 %fusion.9 = bf16[16,1,768]{2,1,0:T(2,128)(2,1)S(1)} fusion(bf16[16,1024,768]{2,1,0:T(8,128)(2,1)} %gather_fusion.6, bf16[16,1024,768]{2,1,0:T(8,128)(2,1)} %gather_fusion.5, bf16[16,1024,768]{2,1,0:T(8,128)(2,1)} %gather_fusion.4, pred[16]{0:T(512)(128)(4,1)S(1)} %compare_and_fusion, bf16[16,3072,1]{1,0,2:T(8,128)(2,1)S(1)} %fusion.35), kind=kOutput, calls=%fused_computation.18 | convolution fusion | flops 339738624 | bytes 75620368 | tf_op jit(solution)/shard_map/bf,bfd->bd/dot_general | solution.py:99
  584.7 0.7 add_convert_fusion
  (44 shorter events, 0.4 us)
Async XLA Ops:
  7.2 72.3 %copy-start.9 = (s32[16]{0:T(128)S(1)}, s32[16]{0:T(128)}, u32[]{:S(2)}) copy-start(s32[16]{0:T(128)} %param.26) | copy-start | bytes 196
  7.2 34.9 %copy-start.10 = (s32[16]{0:T(128)S(1)}, s32[16]{0:T(128)}, u32[]{:S(2)}) copy-start(s32[16]{0:T(128)} %param.29) | copy-start | bytes 196
  7.2 60.1 %copy-start.8 = (f32[768,1]{0,1:T(1,128)S(1)}, f32[768,1]{0,1:T(1,128)}, u32[]{:S(2)}) copy-start(f32[768,1]{0,1:T(1,128)} %param.39) | copy-start | bytes 9220
  7.2 72.0 %copy-start.3 = (bf16[16,768]{1,0:T(8,128)(2,1)S(1)}, bf16[16,768]{1,0:T(8,128)(2,1)}, u32[]{:S(2)}) copy-start(bf16[16,768]{1,0:T(8,128)(2,1)} %param.21) | copy-start | bytes 73732
  7.2 72.4 %copy-start.5 = (s32[16,384]{1,0:T(8,128)S(1)}, s32[16,384]{1,0:T(8,128)}, u32[]{:S(2)}) copy-start(s32[16,384]{1,0:T(8,128)} %param.27) | copy-start | bytes 73732
  7.2 72.4 %copy-start.4 = (f32[768]{0:T(1024)S(1)}, f32[768]{0:T(1024)}, u32[]{:S(2)}) copy-start(f32[768]{0:T(1024)} %param.30) | copy-start | bytes 9220
  7.2 72.4 %all-gather.12.cloned.1.call-start = ((), (), s32[]{:S(2)}) async-start(), calls=%async_computation.1 | async-start | bytes 1327104 | tf_op jit(solution)/shard_map/all_gather | solution.py:52
  8.0 73.6 %all-gather.14.cloned.1.call-start = ((), (), s32[]{:S(2)}) async-start(), calls=%async_computation.2 | async-start | bytes 1327104 | tf_op jit(solution)/shard_map/all_gather | solution.py:53
  8.7 74.7 %all-gather.10.cloned.1.call-start = ((), (), s32[]{:S(2)}) async-start(), calls=%async_computation | async-start | bytes 1327104 | tf_op jit(solution)/shard_map/all_gather | solution.py:51
  9.4 114.9 %all-gather.16.cloned.1.call-start = ((), (), s32[]{:S(2)}) async-start(), calls=%async_computation.3 | async-start | bytes 1327104 | tf_op jit(solution)/shard_map/all_gather | solution.py:54
  10.0 116.2 %all-gather.18.cloned.1.call-start = ((), (), s32[]{:S(2)}) async-start(), calls=%async_computation.4 | async-start | bytes 1327104 | tf_op jit(solution)/shard_map/all_gather | solution.py:55
  10.6 130.3 %all-gather.20.cloned.1.call-start = ((), (), s32[]{:S(2)}) async-start(), calls=%async_computation.5 | async-start | bytes 1327104 | tf_op jit(solution)/shard_map/all_gather | solution.py:56
  11.2 302.8 %all-gather.22.cloned.1.call-start = ((), (), s32[]{:S(2)}) async-start(), calls=%async_computation.6 | async-start | bytes 42467328 | tf_op jit(solution)/shard_map/all_gather | solution.py:58
  11.9 477.9 %all-gather.24.cloned.1.call-start = ((), (), s32[]{:S(2)}) async-start(), calls=%async_computation.7 | async-start | bytes 42467328 | tf_op jit(solution)/shard_map/all_gather | solution.py:59
  99.7 4.8 copy-start
  115.2 11.0 %copy-start.7 = (f32[768]{0:T(1024)S(1)}, f32[768]{0:T(1024)}, u32[]{:S(2)}) copy-start(f32[768]{0:T(1024)} %param.31) | copy-start | bytes 9220
  128.1 14.7 %copy-start.6 = (f32[768]{0:T(1024)S(1)}, f32[768]{0:T(1024)}, u32[]{:S(2)}) copy-start(f32[768]{0:T(1024)} %param.32) | copy-start | bytes 9220
  142.8 0.8 copy-start.1
  559.2 25.6 %copy-start.2 = (f32[16,768]{1,0:T(8,128)S(1)}, f32[16,768]{1,0:T(8,128)}, u32[]{:S(2)}) copy-start(f32[16,768]{1,0:T(8,128)} %copy-done.1) | copy-start | bytes 147460
  559.2 25.6 %copy-start.11 = (f32[16]{0:T(128)S(1)}, f32[16]{0:T(128)}, u32[]{:S(2)}) copy-start(f32[16]{0:T(128)} %compare_select_fusion.4) | copy-start | bytes 196
Sparse Core Ops, SparseCore 0:
  9.8 20.9 all-gather.11
  32.6 18.2 all-gather.13
  52.7 18.2 all-gather.9
  72.7 18.2 all-gather.15
  92.7 18.0 all-gather.17
  112.5 18.0 all-gather.19
  132.4 181.5 all-gather.21
  315.8 173.9 all-gather.23
where the time goes:
time: 593 us; the launch traced here: 592 us
  waiting for transfers between devices  255 us (43%)
  local copies, waits for them, and re-layouts  178 us (30%)
  matrix products  84.2 us (14%)
  blocking collectives  36.8 us (6%)
  other arithmetic  22.8 us (4%)
  between operations  14.6 us (2%)
    all_gather x1, waiting for transfers between devices, decoder_block(): win_full = gather_ws(w_in, axis=2)  170 us
    all_gather x1, waiting for transfers between devices, decoder_block(): wout_full = gather_ws(w_out, axis=1)  79.7 us
    gather x4, local copies, waits for them, and re-layouts, decoder_block(): jnp.take(wout_full, expert_idx, axis=0)  69.3 us
    gather x4, local copies, waits for them, and re-layouts, decoder_block(): jnp.take(win_full, expert_idx, axis=0)  68.7 us
    gather x1, local copies, waits for them, and re-layouts, self_bias(): pos_bias = jnp.take(rel_bias, jnp.clip(distance, 0, cache_len - 1), axis=1)  27.7 us
    dot_general x1, matrix products, decoder_block(): jnp.einsum('bd,bdf->bf', x_norm, jnp.take(win_full, expert_idx, axis=0),...  27.4 us
    dot_general x1, matrix products, decoder_block(): jnp.einsum('bf,bfd->bd', ffn_hidden, jnp.take(wout_full, expert_idx, axis...  25.6 us
    unnamed x1, blocking collectives  25 us
  transfers between devices with their start and end apart: 8, of which 2 were waited for; matrix products, arithmetic and copies ran while one was open for 31% of the time, Pallas kernels for 0%

commit v1 on v0

v1 whole, which is shorter than its diff:
```python
import functools
import jax
import jax.numpy as jnp
from jax import lax
from jax.sharding import PartitionSpec as P
from jax.experimental import pallas as pl
from jax.experimental.pallas import tpu as pltpu

EPSILON = 1e-6
NEG_BIG = -1e30
LANES = 128
GROUP = 2
PIECES = 2
NT = (((1,), (1,)), ((), ()))
MESH = pl.DeviceIdType.MESH
VMEM = pl.BlockSpec(memory_space=pltpu.VMEM)
HBM = pl.BlockSpec(memory_space=pltpu.HBM)
SMEM = pl.BlockSpec(memory_space=pltpu.SMEM)


def hbm(x):
    return pltpu.with_memory_space_constraint(x, pltpu.HBM)


def rms_norm(hidden, scale):
    hid_f32 = hidden.astype(jnp.float32)
    inv_rms = lax.rsqrt(jnp.mean(hid_f32 * hid_f32, axis=-1, keepdims=True) + EPSILON)
    return (hid_f32 * inv_rms * scale).astype(jnp.bfloat16)


def entry_barrier(me, n):
    barrier = pltpu.get_barrier_semaphore()
    for k in range(1, n):
        pl.semaphore_signal(barrier, inc=1, device_id={'ws': lax.rem(me + k, n)}, device_id_type=MESH)
    pl.semaphore_wait(barrier, n - 1)


def remote(src, dst, send_sem, recv_sem, peer):
    return pltpu.make_async_remote_copy(src_ref=src, dst_ref=dst, send_sem=send_sem, recv_sem=recv_sem,
                                        device_id={'ws': peer}, device_id_type=MESH)


def reverse_lanes(x):
    size = x.shape[-1]
    lane = lax.broadcasted_iota(jnp.int32, x.shape, 1)
    step = 1
    while step < size:
        x = jnp.where((lane & step) != 0, pltpu.roll(x, step, 1), pltpu.roll(x, size - step, 1))
        step *= 2
    return x


def gather_kernel(n, hid, eid, ln, bias, wr, wq, wk, wv, wo, wqc, woc, sk, sv, ck, cv,
                  qkv, eid_all, wr_all, bias_rev, wo_all, wqc_all, woc_all, *rest):
    caches, (hall, wqkv, snd, loc_sem, s1, r1, s2, r2, sw, rw) = rest[:4 * PIECES], rest[4 * PIECES:]
    me = lax.axis_index('ws')
    rows, width = hid.shape
    cols = wq.shape[0]
    core, xpos, ypos = lax.rem(me, 2), lax.rem(me // 2, 2), me // 4
    pair = me + 1 - 2 * core
    xnb = me + 2 - 4 * xpos
    ynb = me + 4 - 8 * ypos
    diag = me + 2 - 4 * xpos + 4 - 8 * ypos

    locals_ = []

    def local(src, dst):
        copy = pltpu.make_async_copy(src, dst, loc_sem.at[len(locals_)])
        copy.start()
        locals_.append(copy)
        return copy

    def load_cache(i, src):
        size = src.shape[0] // PIECES
        for t in range(PIECES):
            local(src.at[pl.ds(t * size, size)], caches[i * PIECES + t])

    proj = [local(w, wqkv.at[i]) for i, w in enumerate((wq, wk, wv))]
    for r in range(rows):
        eid_all[me, r:r + 1, :] = jnp.full((1, LANES), eid[r], jnp.int32)
    wr_all[me] = wr[...]
    hall[me] = hid[...]
    entry_barrier(me, n)

    first = []
    for k in range(1, n):
        peer = lax.rem(me + k, n)
        first.append(remote(hid, hall.at[me], s1.at[k - 1, 0], r1.at[k - 1, 0], peer))
        first[-1].start()
    for k in range(1, n):
        peer = lax.rem(me + k, n)
        first.append(remote(eid_all.at[me], eid_all.at[me], s1.at[k - 1, 1], r1.at[k - 1, 1], peer))
        first[-1].start()
        first.append(remote(wr, wr_all.at[me], s1.at[k - 1, 2], r1.at[k - 1, 2], peer))
        first[-1].start()

    fulls = ((wo, wo_all), (wqc, wqc_all), (woc, woc_all))
    half = cols // 2
    to_x, to_y, to_p = [], [], []
    sent = []

    def own_share(i):
        src, dst = fulls[i]
        at = dst.at[pl.ds(pl.multiple_of(me * cols, cols), cols)]
        to_x.append(remote(src, at, sw.at[0, i], rw.at[0, i], xnb))
        to_y.append(remote(src, at, sw.at[1, i], rw.at[1, i], ynb))
        to_p.append(remote(src, at, sw.at[2, i], rw.at[2, i], pair))
        for c in (to_x[-1], to_y[-1], to_p[-1]):
            c.start()
            sent.append(c)
        local(src, at)

    own_share(0)
    load_cache(0, sk)
    load_cache(1, sv)
    bias_rev[...] = reverse_lanes(jnp.concatenate(
        [bias[...], jnp.zeros((bias_rev.shape[0] - bias.shape[0], bias.shape[1]), jnp.float32)], axis=0))

    for c in first[:n - 1]:
        c.wait_recv()
    for c in proj:
        c.wait()
    x_norm = rms_norm(hall[...].reshape(n * rows, width), ln[...])
    for i in range(3):
        y = lax.dot_general(x_norm, wqkv[i], NT, preferred_element_type=jnp.float32)
        snd[:, i] = y.astype(jnp.bfloat16).reshape(n, rows, cols)
    second = []
    for k in range(1, n):
        peer = lax.rem(me + k, n)
        second.append(remote(snd.at[peer], qkv.at[me], s2.at[k - 1], r2.at[k - 1], peer))
        second[-1].start()
    qkv[me] = snd[me]
    own_share(1)
    own_share(2)
    load_cache(2, ck)
    load_cache(3, cv)

    def block(ref, dev, lo, size):
        return ref.at[pl.ds(pl.multiple_of(dev * cols + lo, half), size)]

    def forward(src_dev, lo, size, i, slot, peer):
        dst = fulls[i][1]
        c = remote(block(dst, src_dev, lo, size), block(dst, src_dev, lo, size), sw.at[slot, i], rw.at[slot, i], peer)
        c.start()
        sent.append(c)
        return c

    relay_y, relay_x, pairs = [], [], []
    for i in range(3):
        to_x[i].wait_recv()
        relay_y.append(forward(xnb, 0, half, i, 3, ynb))
        pairs.append(forward(xnb, 0, cols, i, 4, pair))
        to_y[i].wait_recv()
        relay_x.append(forward(ynb, half, half, i, 5, xnb))
        pairs.append(forward(ynb, 0, cols, i, 6, pair))
        if i:
            relay_y[i - 1].wait_recv()
            pairs.append(forward(diag, 0, half, i - 1, 7, pair))
            relay_x[i - 1].wait_recv()
            pairs.append(forward(diag, half, half, i - 1, 8, pair))
    relay_y[2].wait_recv()
    pairs.append(forward(diag, 0, half, 2, 7, pair))
    relay_x[2].wait_recv()
    pairs.append(forward(diag, half, half, 2, 8, pair))

    for c in first[n - 1:]:
        c.wait_recv()
    for c in second:
        c.wait_recv()
    for c in to_p + pairs:
        c.wait_recv()
    for c in first + second + sent:
        c.wait_send()
    for c in locals_[3:]:
        c.wait()


def attn_kernel(pos, hid, qkv, bias_rev, mask, ln_c, ln_f, wo, wqc, woc, *rest):
    cross, (h2_out, x_out, nk, nv), self_kv, (q_sc, ctx_sc, kt_sc, vt_sc, out_sem) = (
        rest[2 * PIECES:4 * PIECES], rest[4 * PIECES:4 * PIECES + 4], rest[4 * PIECES + 4:-5], rest[-5:])
    n, _, rows, cols = qkv.shape
    width = hid.shape[1]
    heads = bias_rev.shape[0]
    head_dim = 64
    self_len = nk.shape[2]
    piece = rows // PIECES
    f32 = jnp.float32
    head_of = lax.broadcasted_iota(jnp.int32, (heads, width), 1) // head_dim
    head_mask = head_of == lax.broadcasted_iota(jnp.int32, (heads, width), 0)
    lane = lax.broadcasted_iota(jnp.int32, (1, LANES), 1)
    key_pos = lax.broadcasted_iota(jnp.int32, (1, self_len), 1)

    def assemble(i):
        return jnp.concatenate([qkv[p, i].astype(f32) for p in range(n)], axis=1)

    q_sc[...] = assemble(0)
    for i, ref in ((1, kt_sc), (2, vt_sc)):
        padded = jnp.concatenate([assemble(i), jnp.zeros((LANES - rows, width), f32)], axis=0)
        cols_t = padded.T
        for g in range(rows // GROUP):
            shifted = cols_t if g == 0 else pltpu.roll(cols_t, LANES - g * GROUP, 1)
            ref[g] = shifted.astype(jnp.bfloat16)

    def softmax(s):
        e = jnp.exp(s - jnp.max(s, axis=-1, keepdims=True))
        return (e / jnp.sum(e, axis=-1, keepdims=True)).astype(jnp.bfloat16)

    def heads_q(b):
        return jnp.where(head_mask, q_sc[pl.ds(b, 1), :], 0.0).astype(jnp.bfloat16)

    def context(b, probs, vals):
        o = lax.dot_general(probs, vals, NT, preferred_element_type=f32)
        ctx_sc[pl.ds(b, 1), :] = jnp.sum(jnp.where(head_mask, o, 0.0), axis=0, keepdims=True)

    for t in range(PIECES):
        keys, vals = self_kv[t], self_kv[PIECES + t]

        @pl.loop(0, piece // GROUP)
        def _(i):
            g = t * (piece // GROUP) + i
            for j in range(GROUP):
                r = i * GROUP + j
                p = pos[g * GROUP + j]
                win = pl.ds(pl.multiple_of((p // LANES) * LANES, LANES), LANES)
                hit = lane == p % LANES
                for cache, new in ((keys, kt_sc), (vals, vt_sc)):
                    cache[r, :, win] = jnp.where(hit, new[g, :, j:j + 1], cache[r, :, win])
            for j in range(GROUP):
                b, r = g * GROUP + j, i * GROUP + j
                p = pos[b]
                s = jnp.dot(heads_q(b), keys[r], preferred_element_type=f32)
                s = s + jnp.where(key_pos <= p, pltpu.roll(bias_rev[...], lax.rem(p + 1, self_len), 1), NEG_BIG)
                context(b, softmax(s), vals[r])
            for j in range(GROUP):
                b, r = g * GROUP + j, i * GROUP + j
                pltpu.make_async_copy(keys.at[r], nk.at[b], out_sem.at[0, b]).start()
                pltpu.make_async_copy(vals.at[r], nv.at[b], out_sem.at[1, b]).start()

    def project(x, w):
        return lax.dot_general(x, w[...], NT, preferred_element_type=f32)

    h1 = (hid[...].astype(f32) + project(ctx_sc[...].astype(jnp.bfloat16), wo)).astype(jnp.bfloat16)
    q_sc[...] = project(rms_norm(h1, ln_c[...]), wqc).astype(jnp.bfloat16).astype(f32)

    for t in range(PIECES):
        keys, vals = cross[t], cross[PIECES + t]

        @pl.loop(0, piece // GROUP)
        def _(i):
            for j in range(GROUP):
                r = i * GROUP + j
                b = t * piece + r
                s = jnp.dot(heads_q(b), keys[r], preferred_element_type=f32)
                s = s + jnp.where(mask[pl.ds(b, 1), :] == 1, 0.0, NEG_BIG)
                context(b, softmax(s), vals[r])

    h2 = (h1.astype(f32) + project(ctx_sc[...].astype(jnp.bfloat16), woc)).astype(jnp.bfloat16)
    h2_out[...] = h2
    x_out[...] = rms_norm(h2, ln_f[...])

    for b in range(rows):
        t, r = b // piece, b % piece
        pltpu.make_async_copy(self_kv[t].at[r], nk.at[b], out_sem.at[0, b]).wait()
        pltpu.make_async_copy(self_kv[PIECES + t].at[r], nv.at[b], out_sem.at[1, b]).wait()


def ffn_kernel(n, capacity, x, h2, eid_all, wr_all, win, wout, out,
               xall, win_v, wout_v, part, acc, loc_sem, s1, r1, s2, r2):
    me = lax.axis_index('ws')
    rows, width = x.shape
    experts, _, hidden_units = win.shape
    group_rows = n * rows
    f32 = jnp.float32
    loads = [pltpu.make_async_copy(win, win_v, loc_sem.at[0]), pltpu.make_async_copy(wout, wout_v, loc_sem.at[1])]
    for c in loads:
        c.start()
    xall[me] = x[...]
    entry_barrier(me, n)
    first = []
    for k in range(1, n):
        peer = lax.rem(me + k, n)
        first.append(remote(x, xall.at[me], s1.at[k - 1], r1.at[k - 1], peer))
        first[-1].start()

    logits = [jnp.sum(x[...].astype(f32) * wr_all[e], axis=-1, keepdims=True) for e in range(experts)]
    top = functools.reduce(jnp.maximum, logits)
    exps = [jnp.exp(l - top) for l in logits]
    total = functools.reduce(jnp.add, exps)
    eid = eid_all[...].reshape(group_rows, LANES)
    own = eid_all[me]
    own_col = own[:, 0:1]
    chosen = functools.reduce(jnp.add, [jnp.where(own_col == e, exps[e], 0.0) for e in range(experts)])
    across = eid.astype(f32).T[0:1, :].astype(jnp.int32)
    row_ids = me * rows + lax.broadcasted_iota(jnp.int32, (rows, group_rows), 0)
    earlier = (across == own_col) & (lax.broadcasted_iota(jnp.int32, (rows, group_rows), 1) < row_ids)
    slot = jnp.sum(jnp.where(earlier, 1.0, 0.0), axis=1, keepdims=True)
    keep_gate = jnp.where(slot < capacity, chosen / total, 0.0)

    for c in first:
        c.wait_recv()
    for c in loads:
        c.wait()
    xs = xall[...].reshape(group_rows, width)
    eid_col = eid[:, 0:1]
    y = jnp.zeros((group_rows, width), f32)
    for e in range(experts):
        u = jnp.dot(xs, win_v[e], preferred_element_type=f32)
        u = jnp.where(eid_col == e, jnp.maximum(u, 0.0), 0.0).astype(jnp.bfloat16)
        y += jnp.dot(u, wout_v[e], preferred_element_type=f32)
    part[...] = y.reshape(n, rows, width)
    second = []
    for k in range(1, n):
        peer = lax.rem(me + k, n)
        second.append(remote(part.at[peer], acc.at[me], s2.at[k - 1], r2.at[k - 1], peer))
        second[-1].start()
    acc[me] = part[me]
    for c in second:
        c.wait_recv()
    y_own = functools.reduce(jnp.add, [acc[p] for p in range(n)]).astype(jnp.bfloat16)
    out[...] = (h2[...].astype(f32) + y_own.astype(f32) * keep_gate).astype(jnp.bfloat16)
    for c in first + second:
        c.wait_send()


def solution(mesh):
    n = mesh.shape['ws']
    row_axes = ('dp', 'ws')
    row_vec = P(row_axes)
    row_mat = P(row_axes, None)
    cache_spec = P(row_axes, None, None, None)
    col_split = P(None, 'ws')
    in_specs = (row_mat, cache_spec, cache_spec, cache_spec, cache_spec, row_vec, row_mat, P(None, None), row_vec,
                P(None), P(None), P(None), col_split, col_split, col_split, col_split, col_split, col_split,
                col_split, P(None, None, 'ws'), P(None, 'ws', None))
    out_specs = (row_mat, cache_spec, cache_spec)

    def decoder_block(hidden, self_k, self_v, cross_k, cross_v, positions, enc_mask, rel_bias, expert_idx,
                      ln_self, ln_cross, ln_ffn, wq_self, wk_self, wv_self, wo_self, wq_cross, wo_cross,
                      w_router, w_in, w_out):
        rows, width = hidden.shape
        heads, head_dim = self_k.shape[1], self_k.shape[3]
        cols = wq_self.shape[1]
        experts, _, units = w_in.shape
        group_rows = rows * n
        capacity = (2 * group_rows + experts - 1) // experts
        bf16, f32, i32 = jnp.bfloat16, jnp.float32, jnp.int32
        pad_heads = 16
        dma = pltpu.SemaphoreType.DMA

        def flat(cache):
            return cache.transpose(0, 1, 3, 2).reshape(rows, heads * head_dim, cache.shape[2])

        sk, sv, ck, cv = (flat(c) for c in (self_k, self_v, cross_k, cross_v))
        pieces = [pltpu.VMEM((rows // PIECES,) + c.shape[1:], bf16) for c in (sk, sv, ck, cv) for _ in range(PIECES)]
        gathered = pl.pallas_call(
            functools.partial(gather_kernel, n),
            out_shape=(
                pltpu.VMEM((n, 3, rows, cols), bf16), pltpu.VMEM((n, rows, LANES), i32), pltpu.VMEM((n, 1, width), f32),
                pltpu.VMEM((pad_heads, rel_bias.shape[1]), f32),
                pltpu.VMEM((n * cols, width), bf16), pltpu.VMEM((n * cols, width), bf16), pltpu.VMEM((n * cols, width), bf16),
                *pieces),
            in_specs=[VMEM, SMEM, VMEM, VMEM, VMEM] + [HBM] * 10,
            out_specs=(VMEM,) * (7 + len(pieces)),
            scratch_shapes=[pltpu.VMEM((n, rows, width), bf16), pltpu.VMEM((3, cols, width), bf16),
                            pltpu.VMEM((n, 3, rows, cols), bf16), dma((6 + 4 * PIECES,)),
                            dma((n - 1, 3)), dma((n - 1, 3)), dma((n - 1,)), dma((n - 1,)), dma((9, 3)), dma((9, 3))],
            compiler_params=pltpu.CompilerParams(collective_id=0, has_side_effects=True, vmem_limit_bytes=7 << 20),
            name='gather')(hidden, expert_idx, ln_self.reshape(1, width), rel_bias, w_router.T,
                           wq_self.T, wk_self.T, wv_self.T, wo_self.T, wq_cross.T, wo_cross.T, hbm(sk), hbm(sv), hbm(ck), hbm(cv))
        qkv, eid_all, wr_all, bias_rev, wo_all, wqc_all, woc_all, *caches = gathered

        h2, x, new_k, new_v, *_ = pl.pallas_call(
            attn_kernel,
            out_shape=(pltpu.VMEM((rows, width), bf16), pltpu.VMEM((rows, width), bf16),
                       pltpu.HBM(sk.shape, bf16), pltpu.HBM(sv.shape, bf16),
                       *pieces[:2 * PIECES]),
            in_specs=[SMEM] + [VMEM] * (9 + len(pieces)),
            out_specs=(VMEM, VMEM, HBM, HBM) + (VMEM,) * (2 * PIECES),
            input_output_aliases={10 + t: 4 + t for t in range(2 * PIECES)},
            scratch_shapes=[pltpu.VMEM((rows, width), f32), pltpu.VMEM((rows, width), f32),
                            pltpu.VMEM((rows // GROUP, width, LANES), bf16), pltpu.VMEM((rows // GROUP, width, LANES), bf16),
                            dma((2, rows))],
            compiler_params=pltpu.CompilerParams(vmem_limit_bytes=7 << 20),
            name='attend')(positions, hidden, qkv, bias_rev, enc_mask, ln_cross.reshape(1, width), ln_ffn.reshape(1, width),
                           wo_all, wqc_all, woc_all, *caches)

        hidden_out = pl.pallas_call(
            functools.partial(ffn_kernel, n, capacity),
            out_shape=jax.ShapeDtypeStruct((rows, width), bf16),
            in_specs=[VMEM] * 4 + [HBM] * 2,
            out_specs=VMEM,
            scratch_shapes=[pltpu.VMEM((n, rows, width), bf16), pltpu.VMEM(w_in.shape, bf16), pltpu.VMEM(w_out.shape, bf16),
                            pltpu.VMEM((n, rows, width), f32), pltpu.VMEM((n, rows, width), f32), dma((2,)),
                            dma((n - 1,)), dma((n - 1,)), dma((n - 1,)), dma((n - 1,))],
            compiler_params=pltpu.CompilerParams(collective_id=1, has_side_effects=True, vmem_limit_bytes=20 << 20),
            name='experts')(x, h2, eid_all, wr_all, hbm(w_in), hbm(w_out))

        def unflat(cache):
            return cache.reshape(rows, heads, head_dim, cache.shape[2]).transpose(0, 1, 3, 2)

        return hidden_out, unflat(new_k), unflat(new_v)

    return jax.shard_map(decoder_block, mesh=mesh, in_specs=in_specs, out_specs=out_specs, check_vma=False)
```

time: 593 us -> 80.1 us (0.14)
  waiting for transfers between devices: 255 us -> 0 us
  local copies, waits for them, and re-layouts: 178 us -> 11 us
  matrix products: 84.2 us -> 0 us
  Pallas kernels: 0 us -> 68 us
  blocking collectives: 36.8 us -> 0 us
  other arithmetic: 22.8 us -> 0 us
  between operations: 14.6 us -> 0.68 us
    all_gather x8 -> x0, waiting for transfers between devices: 250 us -> none  [the longest x1 170 us: decoder_block(): win_full = gather_ws(w_in, axis=2)]
    gather x9 -> x0, local copies, waits for them, and re-layouts: 166 us -> none  [the longest x4 69.3 us: decoder_block(): jnp.take(wout_full, expert_idx, axis=0)]
    dot_general x13 -> x0, matrix products: 84.2 us -> none  [the longest x1 27.4 us: decoder_block(): jnp.einsum('bd,bdf->bf', x_norm, jnp.take(win_full, expert_idx, axis=0),...]
    pallas_call x0 -> x3, Pallas kernels: none -> 68 us  [the longest x1 28.6 us: decoder_block(): pl.pallas_call(functools.partial(gather_kernel, n), out_shape=(pltpu.VMEM...]
    unnamed x1 -> x0, blocking collectives: 25 us -> none
    select_n x4 -> x0, other arithmetic: 15 us -> none  [the longest x1 14.4 us: decoder_block(): new_self_v = jnp.where(write_mask, v_new[:, :, None, :], self_v)]
    all_gather x1 -> x0, blocking collectives: 11.8 us -> none  [decoder_block(): router_full = gather_ws(w_router, axis=1)]
  transfers between devices with their start and end apart: 8 -> 0, of which waited for: 2 -> 0; matrix products, arithmetic and copies ran while one was open for 31% -> 0% of each run, Pallas kernels for 0% -> 0%
where the time goes in v1:
time: 80.1 us; the launch traced here: 79.7 us
  Pallas kernels  68 us (85%)
  local copies, waits for them, and re-layouts  11 us (14%)
    pallas_call x1, Pallas kernels, decoder_block(): pl.pallas_call(functools.partial(gather_kernel, n), out_shape=(pltpu.VMEM...  28.6 us
    pallas_call x1, Pallas kernels, decoder_block(): pl.pallas_call(attn_kernel, out_shape=(pltpu.VMEM((rows, width), bf16), p...  25.5 us
    pallas_call x1, Pallas kernels, decoder_block(): pl.pallas_call(functools.partial(ffn_kernel, n, capacity), out_shape=jax....  14 us
    unnamed x25, local copies, waits for them, and re-layouts  8.91 us

profile of v1, /device:TPU:0, one launch (start us, length us, event | category | flops | bytes accessed | tf_op | source)
XLA Modules:
  0.0 79.7 jit_solution(13979233375000681294)
XLA Ops:
  0.6 0.7 reshape.33.ln
  1.3 0.7 reshape.38.ln_c
  2.0 0.7 reshape.39.ln_f
  2.7 0.0 copy-start
  2.7 0.9 %copy-done = bf16[768,96]{0,1:T(8,128)(2,1)S(1)} copy-done((bf16[768,96]{0,1:T(8,128)(2,1)S(1)}, bf16[768,96]{0,1:T(8,128)(2,1)}, u32[]{:S(2)}) %copy-start) | copy-done | bytes 147480
  3.6 0.0 copy-start.1
  3.6 0.9 %copy-done.1 = bf16[768,96]{0,1:T(8,128)(2,1)S(1)} copy-done((bf16[768,96]{0,1:T(8,128)(2,1)S(1)}, bf16[768,96]{0,1:T(8,128)(2,1)}, u32[]{:S(2)}) %copy-start.1) | copy-done | bytes 147480
  4.5 0.0 copy-start.2
  4.5 0.9 %copy-done.2 = bf16[768,96]{0,1:T(8,128)(2,1)S(1)} copy-done((bf16[768,96]{0,1:T(8,128)(2,1)S(1)}, bf16[768,96]{0,1:T(8,128)(2,1)}, u32[]{:S(2)}) %copy-start.2) | copy-done | bytes 147480
  5.4 0.0 copy-start.3
  5.4 0.9 %copy-done.3 = bf16[768,96]{0,1:T(8,128)(2,1)S(1)} copy-done((bf16[768,96]{0,1:T(8,128)(2,1)S(1)}, bf16[768,96]{0,1:T(8,128)(2,1)}, u32[]{:S(2)}) %copy-start.3) | copy-done | bytes 147480
  6.3 0.0 copy-start.4
  6.3 0.9 %copy-done.4 = bf16[768,96]{0,1:T(8,128)(2,1)S(1)} copy-done((bf16[768,96]{0,1:T(8,128)(2,1)S(1)}, bf16[768,96]{0,1:T(8,128)(2,1)}, u32[]{:S(2)}) %copy-start.4) | copy-done | bytes 147480
  7.3 0.0 copy-start.5
  7.3 0.9 %copy-done.5 = bf16[768,96]{0,1:T(8,128)(2,1)S(1)} copy-done((bf16[768,96]{0,1:T(8,128)(2,1)S(1)}, bf16[768,96]{0,1:T(8,128)(2,1)}, u32[]{:S(2)}) %copy-start.5) | copy-done | bytes 147480
  8.2 0.0 copy-start.6
  8.2 0.7 copy-done.6
  8.9 0.0 copy-start.7
  8.9 0.8 copy-done.7
  9.7 0.0 copy-start.9
  9.7 0.7 copy-done.9
  10.3 0.0 copy-start.10
  10.3 0.7 copy-done.10
  11.0 0.0 copy-start.8
  11.0 0.0 copy-start.11
  11.0 28.6 %gather.1 = (bf16[8,3,16,96]{3,2,1,0:T(8,128)(2,1)S(1)}, s32[8,16,128]{2,1,0:T(8,128)S(1)}, f32[8,1,768]{2,1,0:T(1,128)S(1)}, f32[16,512]{1,0:T(8,128)S(1)}, bf1...) custom-call(bf16[16,768]{1,0:T(8,128)(2,1)S(1)} %copy-done.6, ...), custom_call_target="tpu_custom_call" | custom-call | tf_op jit(solution)/shard_map/gather/pallas_call | solution.py:355
  39.6 0.0 copy-done.8
  39.6 0.0 copy-done.11
  39.6 25.5 %attend.1 = (bf16[16,768]{1,0:T(8,128)(2,1)S(1)}, bf16[16,768]{1,0:T(8,128)(2,1)S(1)}, bf16[16,768,512]{2,1,0:T(8,128)(2,1)}, bf16[16,768,512]{2,1,0:T(8,128)(2,...) custom-call(s32[16]{0:T(128)S(1)} %copy-done.11, ...), custom_call_target="tpu_custom_call", output_to_operand_aliasing={{4}: (10, {}), {5}: (11, {}), {6}: (12, {}), {7}: (13, {})} | custom-call | tf_op jit(solution)/shard_map/attend/pallas_call | solution.py:372
  65.1 14.0 %experts.1 = bf16[16,768]{1,0:T(8,128)(2,1)S(1)} custom-call(bf16[16,768]{1,0:T(8,128)(2,1)S(1)} %get-tuple-element.35.x, bf16[16,768]{1,0:T(8,128)(2,1)S(1)} %get-tuple-element.36.h2, s32[8,16,128]{2,1,0:T(8,128)S(1)} %get-tuple-element.37.eid_all, f32[8,1,768]{2,1,0:T(1,128)S(1)} %get-tuple-element.38.wr_all, bf16[8,768,384]{2,1,0:T(8,128)(2,1)} %win.1, ...), custom_call_target="tpu_custom_call" | custom-call | tf_op jit(solution)/shard_map/experts/pallas_call | solution.py:387
  79.0 0.6 copy.33
Async XLA Ops:
  2.7 0.9 %copy-start = (bf16[768,96]{0,1:T(8,128)(2,1)S(1)}, bf16[768,96]{0,1:T(8,128)(2,1)}, u32[]{:S(2)}) copy-start(bf16[768,96]{0,1:T(8,128)(2,1)} %param.33) | copy-start | bytes 442372
  3.6 0.9 %copy-start.1 = (bf16[768,96]{0,1:T(8,128)(2,1)S(1)}, bf16[768,96]{0,1:T(8,128)(2,1)}, u32[]{:S(2)}) copy-start(bf16[768,96]{0,1:T(8,128)(2,1)} %param.34) | copy-start | bytes 442372
  4.5 0.9 %copy-start.2 = (bf16[768,96]{0,1:T(8,128)(2,1)S(1)}, bf16[768,96]{0,1:T(8,128)(2,1)}, u32[]{:S(2)}) copy-start(bf16[768,96]{0,1:T(8,128)(2,1)} %param.35) | copy-start | bytes 442372
  5.4 0.9 %copy-start.3 = (bf16[768,96]{0,1:T(8,128)(2,1)S(1)}, bf16[768,96]{0,1:T(8,128)(2,1)}, u32[]{:S(2)}) copy-start(bf16[768,96]{0,1:T(8,128)(2,1)} %param.36) | copy-start | bytes 442372
  6.3 0.9 %copy-start.4 = (bf16[768,96]{0,1:T(8,128)(2,1)S(1)}, bf16[768,96]{0,1:T(8,128)(2,1)}, u32[]{:S(2)}) copy-start(bf16[768,96]{0,1:T(8,128)(2,1)} %param.37) | copy-start | bytes 442372
  7.3 0.9 %copy-start.5 = (bf16[768,96]{0,1:T(8,128)(2,1)S(1)}, bf16[768,96]{0,1:T(8,128)(2,1)}, u32[]{:S(2)}) copy-start(bf16[768,96]{0,1:T(8,128)(2,1)} %param.38) | copy-start | bytes 442372
  8.2 0.7 copy-start.6
  8.9 0.8 copy-start.7
  9.7 0.7 copy-start.9
  10.3 0.7 copy-start.10
  11.0 28.6 %copy-start.8 = (s32[16,384]{1,0:T(8,128)S(1)}, s32[16,384]{1,0:T(8,128)}, u32[]{:S(2)}) copy-start(s32[16,384]{1,0:T(8,128)} %mask.1) | copy-start | bytes 73732
  11.0 28.6 %copy-start.11 = (s32[16]{0:T(128)S(1)}, s32[16]{0:T(128)}, u32[]{:S(2)}) copy-start(s32[16]{0:T(128)} %pos.1) | copy-start | bytes 196

commit v2 on v1

--- a/solution.py
+++ b/solution.py
@@ -9,7 +9,7 @@
 EPSILON = 1e-6
 NEG_BIG = -1e30
 LANES = 128
-GROUP = 2
+GROUP = 4
 PIECES = 2
 NT = (((1,), (1,)), ((), ()))
 MESH = pl.DeviceIdType.MESH
@@ -50,12 +50,29 @@
     return x
 
 
-def gather_kernel(n, hid, eid, ln, bias, wr, wq, wk, wv, wo, wqc, woc, sk, sv, ck, cv,
-                  qkv, eid_all, wr_all, bias_rev, wo_all, wqc_all, woc_all, *rest):
-    caches, (hall, wqkv, snd, loc_sem, s1, r1, s2, r2, sw, rw) = rest[:4 * PIECES], rest[4 * PIECES:]
+def load_row(src, dst, sem):
+    return pltpu.make_async_copy(src, dst.at[0], sem)
+
+
+def head_mask_of(heads, width, head_dim):
+    lane = lax.broadcasted_iota(jnp.int32, (heads, width), 1)
+    return lane // head_dim == lax.broadcasted_iota(jnp.int32, (heads, width), 0)
+
+
+def project(x, w):
+    return lax.dot_general(x, w, NT, preferred_element_type=jnp.float32)
+
+
+def gather_kernel(n, head_dim, hid, pos, eid, ln_s, ln_c, bias, wr, wq, wk, wv, wo, wqc, woc, sk, sv, ck, cv,
+                  h1_out, qc_out, kv_out, eid_all, wr_all, wo_all, wqc_all, woc_all, *rest):
+    caches = rest[:4 * PIECES]
+    (hid_v, pos_s, eid_s, ln_sv, ln_cv, bias_v, hall, wqkv, snd, qkv, q_sc, s_sc, p_sc, b_sc, pn_sc, ctx_sc,
+     loc_sem, s1, r1, s2, r2, sw, rw) = rest[4 * PIECES:]
     me = lax.axis_index('ws')
     rows, width = hid.shape
     cols = wq.shape[0]
+    heads, length = b_sc.shape[1:]
+    f32 = jnp.float32
     core, xpos, ypos = lax.rem(me, 2), lax.rem(me // 2, 2), me // 4
     pair = me + 1 - 2 * core
     xnb = me + 2 - 4 * xpos
@@ -75,31 +92,23 @@
         for t in range(PIECES):
             local(src.at[pl.ds(t * size, size)], caches[i * PIECES + t])
 
+    small = [local(hid, hid_v), local(wr, wr_all.at[me]), local(eid, eid_s), local(pos, pos_s),
+             local(bias, bias_v), local(ln_s, ln_sv.at[0]), local(ln_c, ln_cv.at[0])]
     proj = [local(w, wqkv.at[i]) for i, w in enumerate((wq, wk, wv))]
-    for r in range(rows):
-        eid_all[me, r:r + 1, :] = jnp.full((1, LANES), eid[r], jnp.int32)
-    wr_all[me] = wr[...]
-    hall[me] = hid[...]
     entry_barrier(me, n)
-
+    for c in small:
+        c.wait()
     first = []
     for k in range(1, n):
         peer = lax.rem(me + k, n)
-        first.append(remote(hid, hall.at[me], s1.at[k - 1, 0], r1.at[k - 1, 0], peer))
-        first[-1].start()
-    for k in range(1, n):
-        peer = lax.rem(me + k, n)
-        first.append(remote(eid_all.at[me], eid_all.at[me], s1.at[k - 1, 1], r1.at[k - 1, 1], peer))
-        first[-1].start()
-        first.append(remote(wr, wr_all.at[me], s1.at[k - 1, 2], r1.at[k - 1, 2], peer))
+        first.append(remote(hid_v, hall.at[me], s1.at[k - 1, 0], r1.at[k - 1, 0], peer))
         first[-1].start()
 
     fulls = ((wo, wo_all), (wqc, wqc_all), (woc, woc_all))
     half = cols // 2
     to_x, to_y, to_p = [], [], []
     sent = []
-
-    def own_share(i):
+    for i in range(3):
         src, dst = fulls[i]
         at = dst.at[pl.ds(pl.multiple_of(me * cols, cols), cols)]
         to_x.append(remote(src, at, sw.at[0, i], rw.at[0, i], xnb))
@@ -109,31 +118,47 @@
             c.start()
             sent.append(c)
         local(src, at)
-
-    own_share(0)
     load_cache(0, sk)
     load_cache(1, sv)
-    bias_rev[...] = reverse_lanes(jnp.concatenate(
-        [bias[...], jnp.zeros((bias_rev.shape[0] - bias.shape[0], bias.shape[1]), jnp.float32)], axis=0))
-
-    for c in first[:n - 1]:
+    load_cache(2, ck)
+    load_cache(3, cv)
+    hall[me] = hid_v[...]
+    for r in range(rows):
+        eid_all[me, r:r + 1, :] = jnp.full((1, LANES), eid_s[r], jnp.int32)
+    extra = []
+    for k in range(1, n):
+        peer = lax.rem(me + k, n)
+        extra.append(remote(eid_all.at[me], eid_all.at[me], s1.at[k - 1, 1], r1.at[k - 1, 1], peer))
+        extra[-1].start()
+        extra.append(remote(wr_all.at[me], wr_all.at[me], s1.at[k - 1, 2], r1.at[k - 1, 2], peer))
+        extra[-1].start()
+
+    key_pos = lax.broadcasted_iota(jnp.int32, (1, length), 1)
+    table = reverse_lanes(jnp.concatenate(
+        [bias_v[...], jnp.zeros((heads - bias_v.shape[0], length), f32)], axis=0))
+
+    @pl.loop(0, rows)
+    def _(b):
+        p = jnp.full((1, length), pos_s[b], jnp.int32)
+        turned, step = table, 1
+        while step < length:
+            turned = jnp.where(((p + 1) & step) != 0, pltpu.roll(turned, step, 1), turned)
+            step *= 2
+        b_sc[b] = jnp.where(key_pos <= p, turned, NEG_BIG)
+
+    for c in first:
         c.wait_recv()
     for c in proj:
         c.wait()
-    x_norm = rms_norm(hall[...].reshape(n * rows, width), ln[...])
+    x_norm = rms_norm(hall[...].reshape(n * rows, width), ln_sv[...])
     for i in range(3):
-        y = lax.dot_general(x_norm, wqkv[i], NT, preferred_element_type=jnp.float32)
-        snd[:, i] = y.astype(jnp.bfloat16).reshape(n, rows, cols)
+        snd[:, i] = project(x_norm, wqkv[i]).astype(jnp.bfloat16).reshape(n, rows, cols)
     second = []
     for k in range(1, n):
         peer = lax.rem(me + k, n)
         second.append(remote(snd.at[peer], qkv.at[me], s2.at[k - 1], r2.at[k - 1], peer))
         second[-1].start()
     qkv[me] = snd[me]
-    own_share(1)
-    own_share(2)
-    load_cache(2, ck)
-    load_cache(3, cv)
 
     def block(ref, dev, lo, size):
         return ref.at[pl.ds(pl.multiple_of(dev * cols + lo, half), size)]
@@ -146,72 +171,124 @@
         return c
 
     relay_y, relay_x, pairs = [], [], []
-    for i in range(3):
+
+    def relay(i):
         to_x[i].wait_recv()
         relay_y.append(forward(xnb, 0, half, i, 3, ynb))
         pairs.append(forward(xnb, 0, cols, i, 4, pair))
         to_y[i].wait_recv()
         relay_x.append(forward(ynb, half, half, i, 5, xnb))
         pairs.append(forward(ynb, 0, cols, i, 6, pair))
-        if i:
-            relay_y[i - 1].wait_recv()
-            pairs.append(forward(diag, 0, half, i - 1, 7, pair))
-            relay_x[i - 1].wait_recv()
-            pairs.append(forward(diag, half, half, i - 1, 8, pair))
-    relay_y[2].wait_recv()
-    pairs.append(forward(diag, 0, half, 2, 7, pair))
-    relay_x[2].wait_recv()
-    pairs.append(forward(diag, half, half, 2, 8, pair))
-
-    for c in first[n - 1:]:
-        c.wait_recv()
+
+    def relay_diag(i):
+        relay_y[i].wait_recv()
+        pairs.append(forward(diag, 0, half, i, 7, pair))
+        relay_x[i].wait_recv()
+        pairs.append(forward(diag, half, half, i, 8, pair))
+
+    relay(0)
     for c in second:
         c.wait_recv()
-    for c in to_p + pairs:
+    own_kv = locals_[len(small) + 3 + 3:]
+    for c in own_kv[:2 * PIECES]:
+        c.wait()
+
+    def assemble(i):
+        return jnp.concatenate([qkv[p, i].astype(f32) for p in range(n)], axis=1)
+
+    q_sc[...] = assemble(0)
+    kv_out[0] = assemble(1)
+    kv_out[1] = assemble(2)
+    head_mask = head_mask_of(heads, width, head_dim)
+    piece = rows // PIECES
+
+    def scores(t):
+        @pl.loop(0, piece // GROUP)
+        def _(i):
+            for j in range(GROUP):
+                r = i * GROUP + j
+                b = t * piece + r
+                q = jnp.where(head_mask, q_sc[pl.ds(b, 1), :], 0.0)
+                s_new = jnp.sum(q * kv_out[0, pl.ds(b, 1), :], axis=1, keepdims=True)
+                s = jnp.dot(q.astype(jnp.bfloat16), caches[t][r], preferred_element_type=f32)
+                s_sc[b] = jnp.where(key_pos == pos_s[b], s_new, s) + b_sc[b]
+
+    def softmax():
+        @pl.loop(0, rows // GROUP)
+        def _(i):
+            for j in range(GROUP):
+                b = i * GROUP + j
+                s = s_sc[b]
+                e = jnp.exp(s - jnp.max(s, axis=-1, keepdims=True))
+                probs = (e / jnp.sum(e, axis=-1, keepdims=True)).astype(jnp.bfloat16).astype(f32)
+                hit = key_pos == pos_s[b]
+                p_new = jnp.sum(jnp.where(hit, probs, 0.0), axis=1, keepdims=True)
+                pn_sc[b] = jnp.broadcast_to(p_new, (heads, LANES))
+                p_sc[b] = jnp.where(hit, 0.0, probs).astype(jnp.bfloat16)
+
+    def contexts(t):
+        @pl.loop(0, piece // GROUP)
+        def _(i):
+            for j in range(GROUP):
+                r = i * GROUP + j
+                b = t * piece + r
+                o = project(p_sc[b], caches[PIECES + t][r])
+                o = o + pn_sc[b, :, 0:1] * kv_out[1, pl.ds(b, 1), :]
+                ctx_sc[pl.ds(b, 1), :] = jnp.sum(jnp.where(head_mask, o, 0.0), axis=0, keepdims=True)
+
+    scores(0)
+    relay(1)
+    scores(1)
+    softmax()
+    relay_diag(0)
+    contexts(0)
+    relay(2)
+    relay_diag(1)
+    contexts(1)
+    relay_diag(2)
+
+    def wait_weight(i):
+        to_p[i].wait_recv()
+        for c in pairs_of(i):
+            c.wait_recv()
+        locals_[len(small) + 3 + i].wait()
+
+    def pairs_of(i):
+        return [pairs[k] for k in order[i]]
+
+    order = ([0, 1, 4, 5], [2, 3, 8, 9], [6, 7, 10, 11])
+    wait_weight(0)
+    h1 = (hid_v[...].astype(f32) + project(ctx_sc[...].astype(jnp.bfloat16), wo_all[...])).astype(jnp.bfloat16)
+    h1_out[...] = h1
+    wait_weight(1)
+    qc_out[...] = project(rms_norm(h1, ln_cv[...]), wqc_all[...]).astype(jnp.bfloat16).astype(f32)
+    wait_weight(2)
+    for c in extra:
         c.wait_recv()
-    for c in first + second + sent:
+    for c in first + extra + second + sent:
         c.wait_send()
-    for c in locals_[3:]:
+    for c in own_kv[2 * PIECES:]:
         c.wait()
 
 
-def attn_kernel(pos, hid, qkv, bias_rev, mask, ln_c, ln_f, wo, wqc, woc, *rest):
-    cross, (h2_out, x_out, nk, nv), self_kv, (q_sc, ctx_sc, kt_sc, vt_sc, out_sem) = (
-        rest[2 * PIECES:4 * PIECES], rest[4 * PIECES:4 * PIECES + 4], rest[4 * PIECES + 4:-5], rest[-5:])
-    n, _, rows, cols = qkv.shape
-    width = hid.shape[1]
-    heads = bias_rev.shape[0]
-    head_dim = 64
-    self_len = nk.shape[2]
+def attn_kernel(head_dim, pos, h1, qc, kv, mask, ln_f, woc, *rest):
+    cross, (h2_out, x_out, nk, nv), self_kv, (ln_v, s_sc, p_sc, ctx_sc, kt_sc, vt_sc, ln_sem, out_sem) = (
+        rest[2 * PIECES:4 * PIECES], rest[4 * PIECES:4 * PIECES + 4], rest[4 * PIECES + 4:-8], rest[-8:])
+    rows, width = h1.shape
+    heads = s_sc.shape[1]
     piece = rows // PIECES
     f32 = jnp.float32
-    head_of = lax.broadcasted_iota(jnp.int32, (heads, width), 1) // head_dim
-    head_mask = head_of == lax.broadcasted_iota(jnp.int32, (heads, width), 0)
+    load_ln = pltpu.make_async_copy(ln_f, ln_v.at[0], ln_sem)
+    load_ln.start()
+    head_mask = head_mask_of(heads, width, head_dim)
     lane = lax.broadcasted_iota(jnp.int32, (1, LANES), 1)
-    key_pos = lax.broadcasted_iota(jnp.int32, (1, self_len), 1)
-
-    def assemble(i):
-        return jnp.concatenate([qkv[p, i].astype(f32) for p in range(n)], axis=1)
-
-    q_sc[...] = assemble(0)
-    for i, ref in ((1, kt_sc), (2, vt_sc)):
-        padded = jnp.concatenate([assemble(i), jnp.zeros((LANES - rows, width), f32)], axis=0)
-        cols_t = padded.T
+
+    for i, ref in ((0, kt_sc), (1, vt_sc)):
+        cols_t = jnp.concatenate([kv[i], jnp.zeros((LANES - rows, width), f32)], axis=0).T
         for g in range(rows // GROUP):
             shifted = cols_t if g == 0 else pltpu.roll(cols_t, LANES - g * GROUP, 1)
             ref[g] = shifted.astype(jnp.bfloat16)
 
-    def softmax(s):
-        e = jnp.exp(s - jnp.max(s, axis=-1, keepdims=True))
-        return (e / jnp.sum(e, axis=-1, keepdims=True)).astype(jnp.bfloat16)
-
-    def heads_q(b):
-        return jnp.where(head_mask, q_sc[pl.ds(b, 1), :], 0.0).astype(jnp.bfloat16)
-
-    def context(b, probs, vals):
-        o = lax.dot_general(probs, vals, NT, preferred_element_type=f32)
-        ctx_sc[pl.ds(b, 1), :] = jnp.sum(jnp.where(head_mask, o, 0.0), axis=0, keepdims=True)
-
     for t in range(PIECES):
         keys, vals = self_kv[t], self_kv[PIECES + t]
 
@@ -220,44 +297,42 @@
             g = t * (piece // GROUP) + i
             for j in range(GROUP):
                 r = i * GROUP + j
-                p = pos[g * GROUP + j]
+                b = t * piece + r
+                q = jnp.where(head_mask, qc[pl.ds(b, 1), :], 0.0).astype(jnp.bfloat16)
+                s = jnp.dot(q, cross[t][r], preferred_element_type=f32)
+                s_sc[b] = s + jnp.where(mask[pl.ds(b, 1), :] == 1, 0.0, NEG_BIG)
+                p = pos[b]
                 win = pl.ds(pl.multiple_of((p // LANES) * LANES, LANES), LANES)
                 hit = lane == p % LANES
                 for cache, new in ((keys, kt_sc), (vals, vt_sc)):
                     cache[r, :, win] = jnp.where(hit, new[g, :, j:j + 1], cache[r, :, win])
             for j in range(GROUP):
-                b, r = g * GROUP + j, i * GROUP + j
-                p = pos[b]
-                s = jnp.dot(heads_q(b), keys[r], preferred_element_type=f32)
-                s = s + jnp.where(key_pos <= p, pltpu.roll(bias_rev[...], lax.rem(p + 1, self_len), 1), NEG_BIG)
-                context(b, softmax(s), vals[r])
-            for j in range(GROUP):
-                b, r = g * GROUP + j, i * GROUP + j
+                r = i * GROUP + j
+                b = t * piece + r
                 pltpu.make_async_copy(keys.at[r], nk.at[b], out_sem.at[0, b]).start()
                 pltpu.make_async_copy(vals.at[r], nv.at[b], out_sem.at[1, b]).start()
 
-    def project(x, w):
-        return lax.dot_general(x, w[...], NT, preferred_element_type=f32)
-
-    h1 = (hid[...].astype(f32) + project(ctx_sc[...].astype(jnp.bfloat16), wo)).astype(jnp.bfloat16)
-    q_sc[...] = project(rms_norm(h1, ln_c[...]), wqc).astype(jnp.bfloat16).astype(f32)
+    @pl.loop(0, rows // GROUP)
+    def _(i):
+        for j in range(GROUP):
+            b = i * GROUP + j
+            s = s_sc[b]
+            e = jnp.exp(s - jnp.max(s, axis=-1, keepdims=True))
+            p_sc[b] = (e / jnp.sum(e, axis=-1, keepdims=True)).astype(jnp.bfloat16)
 
     for t in range(PIECES):
-        keys, vals = cross[t], cross[PIECES + t]
-
         @pl.loop(0, piece // GROUP)
         def _(i):
             for j in range(GROUP):
                 r = i * GROUP + j
                 b = t * piece + r
-                s = jnp.dot(heads_q(b), keys[r], preferred_element_type=f32)
-                s = s + jnp.where(mask[pl.ds(b, 1), :] == 1, 0.0, NEG_BIG)
-                context(b, softmax(s), vals[r])
-
-    h2 = (h1.astype(f32) + project(ctx_sc[...].astype(jnp.bfloat16), woc)).astype(jnp.bfloat16)
+                o = project(p_sc[b], cross[PIECES + t][r])
+                ctx_sc[pl.ds(b, 1), :] = jnp.sum(jnp.where(head_mask, o, 0.0), axis=0, keepdims=True)
+
+    h2 = (h1[...].astype(f32) + project(ctx_sc[...].astype(jnp.bfloat16), woc[...])).astype(jnp.bfloat16)
     h2_out[...] = h2
-    x_out[...] = rms_norm(h2, ln_f[...])
-
+    load_ln.wait()
+    x_out[...] = rms_norm(h2, ln_v[...])
     for b in range(rows):
         t, r = b // piece, b % piece
         pltpu.make_async_copy(self_kv[t].at[r], nk.at[b], out_sem.at[0, b]).wait()
@@ -352,37 +427,41 @@
 
         sk, sv, ck, cv = (flat(c) for c in (self_k, self_v, cross_k, cross_v))
         pieces = [pltpu.VMEM((rows // PIECES,) + c.shape[1:], bf16) for c in (sk, sv, ck, cv) for _ in range(PIECES)]
+        length, src_len = sk.shape[2], ck.shape[2]
+        row_bf16, row_f32 = pltpu.VMEM((rows, width), bf16), pltpu.VMEM((rows, width), f32)
+        full = pltpu.VMEM((n * cols, width), bf16)
+        ln_row = pltpu.VMEM((1, width), f32)
+        operands = (hidden, positions, expert_idx, ln_self, ln_cross, rel_bias, w_router.T,
+                    wq_self.T, wk_self.T, wv_self.T, wo_self.T, wq_cross.T, wo_cross.T, sk, sv, ck, cv)
         gathered = pl.pallas_call(
-            functools.partial(gather_kernel, n),
-            out_shape=(
-                pltpu.VMEM((n, 3, rows, cols), bf16), pltpu.VMEM((n, rows, LANES), i32), pltpu.VMEM((n, 1, width), f32),
-                pltpu.VMEM((pad_heads, rel_bias.shape[1]), f32),
-                pltpu.VMEM((n * cols, width), bf16), pltpu.VMEM((n * cols, width), bf16), pltpu.VMEM((n * cols, width), bf16),
-                *pieces),
-            in_specs=[VMEM, SMEM, VMEM, VMEM, VMEM] + [HBM] * 10,
-            out_specs=(VMEM,) * (7 + len(pieces)),
-            scratch_shapes=[pltpu.VMEM((n, rows, width), bf16), pltpu.VMEM((3, cols, width), bf16),
-                            pltpu.VMEM((n, 3, rows, cols), bf16), dma((6 + 4 * PIECES,)),
+            functools.partial(gather_kernel, n, head_dim),
+            out_shape=(row_bf16, row_f32, pltpu.VMEM((2, rows, width), f32),
+                       pltpu.VMEM((n, rows, LANES), i32), pltpu.VMEM((n, 1, width), f32), full, full, full, *pieces),
+            in_specs=[HBM] * len(operands),
+            out_specs=(VMEM,) * (8 + len(pieces)),
+            scratch_shapes=[row_bf16, pltpu.SMEM((rows,), i32), pltpu.SMEM((rows,), i32), ln_row, ln_row,
+                            pltpu.VMEM(rel_bias.shape, f32),
+                            pltpu.VMEM((n, rows, width), bf16), pltpu.VMEM((3, cols, width), bf16),
+                            pltpu.VMEM((n, 3, rows, cols), bf16), pltpu.VMEM((n, 3, rows, cols), bf16), row_f32,
+                            pltpu.VMEM((rows, pad_heads, length), f32), pltpu.VMEM((rows, pad_heads, length), bf16),
+                            pltpu.VMEM((rows, pad_heads, length), f32), pltpu.VMEM((rows, pad_heads, LANES), f32), row_f32,
+                            dma((13 + 4 * PIECES,)),
                             dma((n - 1, 3)), dma((n - 1, 3)), dma((n - 1,)), dma((n - 1,)), dma((9, 3)), dma((9, 3))],
             compiler_params=pltpu.CompilerParams(collective_id=0, has_side_effects=True, vmem_limit_bytes=7 << 20),
-            name='gather')(hidden, expert_idx, ln_self.reshape(1, width), rel_bias, w_router.T,
-                           wq_self.T, wk_self.T, wv_self.T, wo_self.T, wq_cross.T, wo_cross.T, hbm(sk), hbm(sv), hbm(ck), hbm(cv))
-        qkv, eid_all, wr_all, bias_rev, wo_all, wqc_all, woc_all, *caches = gathered
+            name='gather')(*(hbm(x) for x in operands))
+        h1, qc, kv, eid_all, wr_all, _, _, woc_all, *caches = gathered
 
         h2, x, new_k, new_v, *_ = pl.pallas_call(
-            attn_kernel,
-            out_shape=(pltpu.VMEM((rows, width), bf16), pltpu.VMEM((rows, width), bf16),
-                       pltpu.HBM(sk.shape, bf16), pltpu.HBM(sv.shape, bf16),
-                       *pieces[:2 * PIECES]),
-            in_specs=[SMEM] + [VMEM] * (9 + len(pieces)),
+            functools.partial(attn_kernel, head_dim),
+            out_shape=(row_bf16, row_bf16, pltpu.HBM(sk.shape, bf16), pltpu.HBM(sv.shape, bf16), *pieces[:2 * PIECES]),
+            in_specs=[SMEM] + [VMEM] * 4 + [HBM] + [VMEM] * (1 + len(pieces)),
             out_specs=(VMEM, VMEM, HBM, HBM) + (VMEM,) * (2 * PIECES),
-            input_output_aliases={10 + t: 4 + t for t in range(2 * PIECES)},
-            scratch_shapes=[pltpu.VMEM((rows, width), f32), pltpu.VMEM((rows, width), f32),
-                            pltpu.VMEM((rows // GROUP, width, LANES), bf16), pltpu.VMEM((rows // GROUP, width, LANES), bf16),
-                            dma((2, rows))],
+            input_output_aliases={7 + t: 4 + t for t in range(2 * PIECES)},
+            scratch_shapes=[ln_row, pltpu.VMEM((rows, pad_heads, src_len), f32), pltpu.VMEM((rows, pad_heads, src_len), bf16),
+                            row_f32, pltpu.VMEM((rows // GROUP, width, LANES), bf16),
+                            pltpu.VMEM((rows // GROUP, width, LANES), bf16), dma, dma((2, rows))],
             compiler_params=pltpu.CompilerParams(vmem_limit_bytes=7 << 20),
-            name='attend')(positions, hidden, qkv, bias_rev, enc_mask, ln_cross.reshape(1, width), ln_ffn.reshape(1, width),
-                           wo_all, wqc_all, woc_all, *caches)
+            name='attend')(positions, h1, qc, kv, enc_mask, hbm(ln_ffn), woc_all, *caches)
 
         hidden_out = pl.pallas_call(
             functools.partial(ffn_kernel, n, capacity),

time: 80.1 us -> 59.6 us (0.74)
  local copies, waits for them, and re-layouts: 11 us -> 0.62 us
  Pallas kernels: 68 us -> 58.2 us
    pallas_call x2, Pallas kernels: 54 us -> 43.5 us  [the longest x1 32.9 us: decoder_block(): pl.pallas_call(functools.partial(gather_kernel, n, head_dim), out_shape=(...]
    unnamed x25 -> x5, local copies, waits for them, and re-layouts: 8.91 us -> 0.62 us
    reshape x3 -> x0, local copies, waits for them, and re-layouts: 2.07 us -> none  [the longest x1 0.69 us: decoder_block(): ln_self.reshape(1, width)]
where the time goes in v2:
time: 59.6 us; the launch traced here: 59.5 us
  Pallas kernels  58.2 us (98%)
  between operations  0.69 us (1%)
  local copies, waits for them, and re-layouts  0.62 us (1%)
    pallas_call x1, Pallas kernels, decoder_block(): pl.pallas_call(functools.partial(gather_kernel, n, head_dim), out_shape=(...  32.9 us
    pallas_call x1, Pallas kernels, decoder_block(): pl.pallas_call(functools.partial(ffn_kernel, n, capacity), out_shape=jax....  14.7 us
    pallas_call x1, Pallas kernels, decoder_block(): pl.pallas_call(functools.partial(attn_kernel, head_dim), out_shape=(row_b...  10.6 us

profile of v2, /device:TPU:0, one launch (start us, length us, event | category | flops | bytes accessed | tf_op | source)
XLA Modules:
  0.0 59.5 jit_solution(6301838438837089696)
XLA Ops:
  0.6 0.0 copy-start
  0.6 0.0 copy-start.1
  0.7 32.9 %gather.1 = (bf16[16,768]{1,0:T(8,128)(2,1)S(1)}, f32[16,768]{1,0:T(8,128)S(1)}, f32[2,16,768]{2,1,0:T(8,128)S(1)}, s32[8,16,128]{2,1,0:T(8,128)S(1)}, f32[8,1,7...) custom-call(bf16[16,768]{1,0:T(8,128)(2,1)} %hid.1, ...), custom_call_target="tpu_custom_call" | custom-call | tf_op jit(solution)/shard_map/gather/pallas_call | solution.py:436
  33.6 0.0 copy-done
  33.6 0.0 copy-done.1
  33.6 10.6 %attend.1 = (bf16[16,768]{1,0:T(8,128)(2,1)S(1)}, bf16[16,768]{1,0:T(8,128)(2,1)S(1)}, bf16[16,768,512]{2,1,0:T(8,128)(2,1)}, bf16[16,768,512]{2,1,0:T(8,128)(2,...) custom-call(s32[16]{0:T(128)S(1)} %copy-done.1, ...), custom_call_target="tpu_custom_call", output_to_operand_aliasing={{4}: (7, {}), {5}: (8, {}), {6}: (9, {}), {7}: (10, {})} | custom-call | tf_op jit(solution)/shard_map/attend/pallas_call | solution.py:454
  44.2 14.7 %experts.1 = bf16[16,768]{1,0:T(8,128)(2,1)S(1)} custom-call(bf16[16,768]{1,0:T(8,128)(2,1)S(1)} %get-tuple-element.33.x, bf16[16,768]{1,0:T(8,128)(2,1)S(1)} %get-tuple-element.34.h2, s32[8,16,128]{2,1,0:T(8,128)S(1)} %get-tuple-element.35.eid_all, f32[8,1,768]{2,1,0:T(1,128)S(1)} %get-tuple-element.36.wr_all, bf16[8,768,384]{2,1,0:T(8,128)(2,1)} %win.1, ...), custom_call_target="tpu_custom_call" | custom-call | tf_op jit(solution)/shard_map/experts/pallas_call | solution.py:466
  58.9 0.6 %copy.33 = bf16[16,768]{1,0:T(8,128)(2,1)} copy(bf16[16,768]{1,0:T(8,128)(2,1)S(1)} %experts.1) | data formatting | bytes 49152
Async XLA Ops:
  0.6 33.0 %copy-start = (s32[16,384]{1,0:T(8,128)S(1)}, s32[16,384]{1,0:T(8,128)}, u32[]{:S(2)}) copy-start(s32[16,384]{1,0:T(8,128)} %mask.1) | copy-start | bytes 73732
  0.6 33.0 %copy-start.1 = (s32[16]{0:T(128)S(1)}, s32[16]{0:T(128)}, u32[]{:S(2)}) copy-start(s32[16]{0:T(128)} %pos.3) | copy-start | bytes 196

commit v3 on v0

v3 whole, which is shorter than its diff:
```python
import functools
import jax
import jax.numpy as jnp
from jax import lax
from jax.sharding import PartitionSpec as P
from jax.experimental import pallas as pl
from jax.experimental.pallas import tpu as pltpu

EPSILON = 1e-6
NEG_BIG = -1e30
LANES = 128
GROUP = 4
UPDATE = 4
PIECES = 2
NT = (((1,), (1,)), ((), ()))
MESH = pl.DeviceIdType.MESH
VMEM = pl.BlockSpec(memory_space=pltpu.VMEM)
HBM = pl.BlockSpec(memory_space=pltpu.HBM)
SMEM = pl.BlockSpec(memory_space=pltpu.SMEM)


def hbm(x):
    return pltpu.with_memory_space_constraint(x, pltpu.HBM)


def rms_norm(hidden, scale):
    hid_f32 = hidden.astype(jnp.float32)
    inv_rms = lax.rsqrt(jnp.mean(hid_f32 * hid_f32, axis=-1, keepdims=True) + EPSILON)
    return (hid_f32 * inv_rms * scale).astype(jnp.bfloat16)


def entry_barrier(me, n):
    barrier = pltpu.get_barrier_semaphore()
    for k in range(1, n):
        pl.semaphore_signal(barrier, inc=1, device_id={'ws': lax.rem(me + k, n)}, device_id_type=MESH)
    pl.semaphore_wait(barrier, n - 1)


def remote(src, dst, send_sem, recv_sem, peer):
    return pltpu.make_async_remote_copy(src_ref=src, dst_ref=dst, send_sem=send_sem, recv_sem=recv_sem,
                                        device_id={'ws': peer}, device_id_type=MESH)


def reverse_lanes(x):
    size = x.shape[-1]
    lane = lax.broadcasted_iota(jnp.int32, x.shape, 1)
    step = 1
    while step < size:
        x = jnp.where((lane & step) != 0, pltpu.roll(x, step, 1), pltpu.roll(x, size - step, 1))
        step *= 2
    return x


def head_mask_of(heads, width, head_dim):
    lane = lax.broadcasted_iota(jnp.int32, (heads, width), 1)
    return lane // head_dim == lax.broadcasted_iota(jnp.int32, (heads, width), 0)


def project(x, w):
    return lax.dot_general(x, w, NT, preferred_element_type=jnp.float32)


def gather_kernel(n, head_dim, hid, pos, eid, mask, ln_s, ln_c, ln_f, bias, wr, wq, wk, wv, wo, wqc, woc,
                  sk, sv, ck, cv,
                  h2_out, xall, eid_all, wr_all, *rest):
    (kt_out, vt_out), self_kv = rest[:2], rest[2:2 * PIECES + 2]
    (ck_v, cv_v, wo_all, wqc_all, woc_all, hid_v, pos_s, eid_s, mask_v, ln_sv, ln_cv, ln_fv, bias_v, hall, wqkv, snd, qkv,
     q_sc, kv_out, s_sc, p_sc, pn_sc, ctx_sc, loc_sem, send, recv, sw, rw, rp) = rest[2 * PIECES + 2:]
    me = lax.axis_index('ws')
    rows, width = hid.shape
    cols = wq.shape[0]
    heads, length = s_sc.shape[1:]
    src_len = ck.shape[2]
    piece = rows // PIECES
    f32, bf16 = jnp.float32, jnp.bfloat16
    core, xpos, ypos = lax.rem(me, 2), lax.rem(me // 2, 2), me // 4
    pair = me + 1 - 2 * core
    xnb = me + 2 - 4 * xpos
    ynb = me + 4 - 8 * ypos
    diag = me + 2 - 4 * xpos + 4 - 8 * ypos
    peers = [lax.rem(me + k, n) for k in range(1, n)]

    count = []

    def local(src, dst):
        copy = pltpu.make_async_copy(src, dst, loc_sem.at[len(count)])
        copy.start()
        count.append(copy)
        return copy

    small = [local(hid, hid_v), local(wr, wr_all.at[me]), local(eid, eid_s), local(pos, pos_s), local(bias, bias_v),
             local(ln_s, ln_sv.at[0]), local(ln_c, ln_cv.at[0]), local(ln_f, ln_fv.at[0]), local(mask, mask_v)]
    proj = [local(w, wqkv.at[i]) for i, w in enumerate((wq, wk, wv))]
    entry_barrier(me, n)
    for c in small:
        c.wait()
    first = [remote(hid_v, hall.at[me], send.at[0], recv.at[0], p) for p in peers]
    others = pl.ds(0, n - 1)

    def all_of(ref, i):
        return remote(ref.at[others], ref.at[others], send.at[i], recv.at[i], peers[0])

    for c in first:
        c.start()

    fulls = ((wo, wo_all), (wqc, wqc_all), (woc, woc_all))
    half = cols // 2
    to_x, to_y, own_copies = [], [], []

    def own_share(i):
        src, dst = fulls[i]
        at = dst.at[pl.ds(pl.multiple_of(me * cols, cols), cols)]
        to_x.append(remote(src, at, sw.at[i], rw.at[0, i], xnb))
        to_y.append(remote(src, at, sw.at[i], rw.at[1, i], ynb))
        for c in (to_x[-1], to_y[-1], remote(src, at, sw.at[i], rp.at[i], pair)):
            c.start()
        own_copies.append(local(src, at))

    own_share(0)
    load_self = [local(src.at[pl.ds(t * piece, piece)], self_kv[i * PIECES + t])
                 for i, src in enumerate((sk, sv)) for t in range(PIECES)]
    load_cross = [local(ck, ck_v), local(cv.at[pl.ds(0, piece)], cv_v)]
    hall[me] = hid_v[...]
    for r in range(rows):
        eid_all[me, r:r + 1, :] = jnp.full((1, LANES), eid_s[r], jnp.int32)
    for p in peers:
        remote(eid_all.at[me], eid_all.at[me], send.at[1], recv.at[1], p).start()
        remote(wr_all.at[me], wr_all.at[me], send.at[2], recv.at[2], p).start()

    key_pos = lax.broadcasted_iota(jnp.int32, (1, length), 1)
    table = reverse_lanes(jnp.concatenate(
        [bias_v[...], jnp.zeros((heads - bias_v.shape[0], length), f32)], axis=0))

    @pl.loop(0, rows // GROUP)
    def _(i):
        marks = [jnp.full((1, length), pos_s[i * GROUP + j], jnp.int32) for j in range(GROUP)]
        turned, step = [table] * GROUP, 1
        while step < length:
            turned = [jnp.where(((p + 1) & step) != 0, pltpu.roll(t, step, 1), t) for p, t in zip(marks, turned)]
            step *= 2
        for j in range(GROUP):
            s_sc[i * GROUP + j] = jnp.where(key_pos <= marks[j], turned[j], NEG_BIG)

    all_of(hall, 0).wait_recv()
    for c in proj:
        c.wait()
    x_norm = rms_norm(hall[...].reshape(n * rows, width), ln_sv[...])
    for i in range(3):
        snd[:, i] = project(x_norm, wqkv[i]).astype(bf16).reshape(n, rows, cols)
    second = [remote(snd.at[p], qkv.at[me], send.at[3], recv.at[3], p) for p in peers]
    for c in second:
        c.start()
    qkv[me] = snd[me]
    own_share(1)

    def forward(src_dev, lo, size, i, sem, peer):
        dst = fulls[i][1].at[pl.ds(pl.multiple_of(src_dev * cols + lo, half), size)]
        c = remote(dst, dst, sw.at[i], sem, peer)
        c.start()
        return c

    relay_y, relay_x = {}, {}

    def relay(i):
        to_x[i].wait_recv()
        relay_y[i] = forward(xnb, 0, half, i, rw.at[2, i], ynb)
        forward(xnb, 0, cols, i, rp.at[i], pair)
        to_y[i].wait_recv()
        relay_x[i] = forward(ynb, half, half, i, rw.at[3, i], xnb)
        forward(ynb, 0, cols, i, rp.at[i], pair)

    def relay_diag(i):
        relay_y[i].wait_recv()
        forward(diag, 0, half, i, rp.at[i], pair)
        relay_x[i].wait_recv()
        forward(diag, half, half, i, rp.at[i], pair)

    def wait_weight(i):
        theirs = fulls[i][1].at[pl.ds(0, 4 * cols)]
        remote(theirs, theirs, sw.at[i], rp.at[i], pair).wait_recv()
        own_copies[i].wait()

    all_of(qkv, 3).wait_recv()
    for c in load_self:
        c.wait()

    def assemble(i):
        return jnp.concatenate([qkv[p, i].astype(f32) for p in range(n)], axis=1)

    q_sc[...] = assemble(0)
    kv_out[0] = assemble(1)
    kv_out[1] = assemble(2)
    head_mask = head_mask_of(heads, width, head_dim)

    def over_rows(lo, hi, body):
        @pl.loop(0, (hi - lo) // GROUP)
        def _(i):
            for j in range(GROUP):
                body(lo + i * GROUP + j, i * GROUP + j)

    def softmax(s):
        e = jnp.exp(s - jnp.max(s, axis=-1, keepdims=True))
        return (e / jnp.sum(e, axis=-1, keepdims=True)).astype(bf16)

    def store_context(b, o):
        ctx_sc[pl.ds(b, 1), :] = jnp.sum(jnp.where(head_mask, o, 0.0), axis=0, keepdims=True)

    def self_scores(t):
        def body(b, r):
            q = jnp.where(head_mask, q_sc[pl.ds(b, 1), :], 0.0)
            s_new = jnp.sum(q * kv_out[0, pl.ds(b, 1), :], axis=1, keepdims=True)
            s = jnp.dot(q.astype(bf16), self_kv[t][r], preferred_element_type=f32)
            s_sc[b] = jnp.where(key_pos == pos_s[b], s_new, s) + s_sc[b]
        over_rows(t * piece, (t + 1) * piece, body)

    def self_softmax():
        def body(b, r):
            probs = softmax(s_sc[b]).astype(f32)
            hit = key_pos == pos_s[b]
            p_new = jnp.sum(jnp.where(hit, probs, 0.0), axis=1, keepdims=True)
            pn_sc[b] = jnp.broadcast_to(p_new, (heads, LANES))
            p_sc[b] = jnp.where(hit, 0.0, probs).astype(bf16)
        over_rows(0, rows, body)

    def self_context(t):
        def body(b, r):
            o = project(p_sc[b], self_kv[PIECES + t][r])
            store_context(b, o + pn_sc[b, :, 0:1] * kv_out[1, pl.ds(b, 1), :])
        over_rows(t * piece, (t + 1) * piece, body)

    relay(0)
    own_share(2)
    self_scores(0)
    self_scores(1)
    relay(1)
    self_softmax()
    relay_diag(0)
    self_context(0)
    self_context(1)
    relay_diag(1)
    relay(2)

    wait_weight(0)
    h1 = (hid_v[...].astype(f32) + project(ctx_sc[...].astype(bf16), wo_all[...])).astype(bf16)
    wait_weight(1)
    q_sc[...] = project(rms_norm(h1, ln_cv[...]), wqc_all[...]).astype(bf16).astype(f32)
    for c in load_cross:
        c.wait()

    def cross_scores(b, r):
        q = jnp.where(head_mask, q_sc[pl.ds(b, 1), :], 0.0).astype(bf16)
        s_sc[b, :, 0:src_len] = (jnp.dot(q, ck_v[b], preferred_element_type=f32)
                                 + jnp.where(mask_v[pl.ds(b, 1), :] == 1, 0.0, NEG_BIG))

    def cross_softmax(b, r):
        p_sc[b, :, 0:src_len] = softmax(s_sc[b, :, 0:src_len])

    def cross_context(b, r):
        store_context(b, project(p_sc[b, :, 0:src_len], cv_v[b]))

    def cross_context_late(b, r):
        store_context(b, project(p_sc[b, :, 0:src_len], ck_v[r]))

    over_rows(0, piece, cross_scores)
    relay_diag(2)
    load_late = local(cv.at[pl.ds(piece, piece)], ck_v.at[pl.ds(0, piece)])
    over_rows(piece, rows, cross_scores)
    over_rows(0, rows, cross_softmax)
    over_rows(0, piece, cross_context)
    load_late.wait()
    over_rows(piece, rows, cross_context_late)
    wait_weight(2)
    h2 = (h1.astype(f32) + project(ctx_sc[...].astype(bf16), woc_all[...])).astype(bf16)
    xall[me] = rms_norm(h2, ln_fv[...])
    h2_out[...] = h2
    third = [remote(xall.at[me], xall.at[me], send.at[4], recv.at[4], p) for p in peers]
    for c in third:
        c.start()
    for i, ref in enumerate((kt_out, vt_out)):
        cols_t = jnp.concatenate([kv_out[i], jnp.zeros((LANES - rows, width), f32)], axis=0).T
        for g in range(rows // UPDATE):
            shifted = cols_t if g == 0 else pltpu.roll(cols_t, LANES - g * UPDATE, 1)
            ref[g] = shifted.astype(bf16)
    for i, ref in ((1, eid_all), (2, wr_all), (4, xall)):
        all_of(ref, i).wait_recv()
    for i, ref in enumerate((hall, eid_all, wr_all, snd, xall)):
        all_of(ref, i).wait_send()
    for i in range(3):
        moved = fulls[i][1].at[pl.ds(0, 7 * cols)]
        remote(moved, moved, sw.at[i], rp.at[i], pair).wait_send()


def update_kernel(n, capacity, pos, kt, vt, xall, eid_all, wr_all, win, wout, *rest):
    (part, gate, nk, nv), self_kv, (hidden_sc, out_sem) = (
        rest[2 * PIECES:2 * PIECES + 4], rest[2 * PIECES + 4:-2], rest[-2:])
    me = lax.axis_index('ws')
    _, rows, width = xall.shape
    experts, _, units = win.shape
    group_rows = n * rows
    piece = rows // PIECES
    f32 = jnp.float32
    lane = lax.broadcasted_iota(jnp.int32, (1, LANES), 1)

    for t in range(PIECES):
        keys, vals = self_kv[t], self_kv[PIECES + t]

        @pl.loop(0, piece // UPDATE)
        def _(i):
            g = t * (piece // UPDATE) + i
            for j in range(UPDATE):
                r = i * UPDATE + j
                b = t * piece + r
                p = pos[b]
                win_at = pl.ds(pl.multiple_of((p // LANES) * LANES, LANES), LANES)
                hit = lane == p % LANES
                for cache, new in ((keys, kt), (vals, vt)):
                    cache[r, :, win_at] = jnp.where(hit, new[g, :, j:j + 1], cache[r, :, win_at])
            for j in range(UPDATE):
                r = i * UPDATE + j
                b = t * piece + r
                pltpu.make_async_copy(keys.at[r], nk.at[b], out_sem.at[0]).start()
                pltpu.make_async_copy(vals.at[r], nv.at[b], out_sem.at[1]).start()

    eid = eid_all[...].reshape(group_rows, LANES)
    eid_col = eid[:, 0:1]
    xs = xall[...].reshape(group_rows, width)
    for e in range(experts):
        u = jnp.dot(xs, win[e], preferred_element_type=f32)
        hidden_sc[:, e * units:(e + 1) * units] = jnp.where(eid_col == e, jnp.maximum(u, 0.0), 0.0).astype(jnp.bfloat16)
    y = jnp.dot(hidden_sc[...], wout[...].reshape(experts * units, width), preferred_element_type=f32)
    part[...] = y.reshape(n, rows, width)

    x_own = xall[me].astype(f32)
    logits = [jnp.sum(x_own * wr_all[e], axis=-1, keepdims=True) for e in range(experts)]
    top = functools.reduce(jnp.maximum, logits)
    exps = [jnp.exp(l - top) for l in logits]
    total = functools.reduce(jnp.add, exps)
    own_col = eid_all[me][:, 0:1]
    chosen = functools.reduce(jnp.add, [jnp.where(own_col == e, exps[e], 0.0) for e in range(experts)])
    across = eid.astype(f32).T[0:1, :].astype(jnp.int32)
    row_ids = me * rows + lax.broadcasted_iota(jnp.int32, (rows, group_rows), 0)
    earlier = (across == own_col) & (lax.broadcasted_iota(jnp.int32, (rows, group_rows), 1) < row_ids)
    slot = jnp.sum(jnp.where(earlier, 1.0, 0.0), axis=1, keepdims=True)
    gate[...] = jnp.broadcast_to(jnp.where(slot < capacity, chosen / total, 0.0), gate.shape)

    for i, ref in enumerate((nk, nv)):
        pltpu.make_async_copy(ref, ref, out_sem.at[i]).wait()


def reduce_kernel(n, part, gate, h2, out, acc, send, recv):
    me = lax.axis_index('ws')
    f32 = jnp.float32
    entry_barrier(me, n)
    for k in range(1, n):
        peer = lax.rem(me + k, n)
        remote(part.at[peer], acc.at[me], send, recv, peer).start()
    acc[me] = part[me]
    others = pl.ds(0, n - 1)
    copies = remote(part.at[others], acc.at[others], send, recv, lax.rem(me + 1, n))
    copies.wait_recv()
    y_own = functools.reduce(jnp.add, [acc[p] for p in range(n)]).astype(jnp.bfloat16)
    out[...] = (h2[...].astype(f32) + y_own.astype(f32) * gate[:, 0:1]).astype(jnp.bfloat16)
    copies.wait_send()


def solution(mesh):
    n = mesh.shape['ws']
    row_axes = ('dp', 'ws')
    row_vec = P(row_axes)
    row_mat = P(row_axes, None)
    cache_spec = P(row_axes, None, None, None)
    col_split = P(None, 'ws')
    in_specs = (row_mat, cache_spec, cache_spec, cache_spec, cache_spec, row_vec, row_mat, P(None, None), row_vec,
                P(None), P(None), P(None), col_split, col_split, col_split, col_split, col_split, col_split,
                col_split, P(None, None, 'ws'), P(None, 'ws', None))
    out_specs = (row_mat, cache_spec, cache_spec)

    def decoder_block(hidden, self_k, self_v, cross_k, cross_v, positions, enc_mask, rel_bias, expert_idx,
                      ln_self, ln_cross, ln_ffn, wq_self, wk_self, wv_self, wo_self, wq_cross, wo_cross,
                      w_router, w_in, w_out):
        rows, width = hidden.shape
        heads, head_dim = self_k.shape[1], self_k.shape[3]
        cols = wq_self.shape[1]
        experts, _, units = w_in.shape
        group_rows = rows * n
        capacity = (2 * group_rows + experts - 1) // experts
        bf16, f32, i32 = jnp.bfloat16, jnp.float32, jnp.int32
        pad_heads = 16
        dma = pltpu.SemaphoreType.DMA

        def flat(cache):
            return cache.transpose(0, 1, 3, 2).reshape(rows, heads * head_dim, cache.shape[2])

        sk, sv, ck, cv = (flat(c) for c in (self_k, self_v, cross_k, cross_v))
        pieces = [pltpu.VMEM((rows // PIECES,) + c.shape[1:], bf16) for c in (sk, sv) for _ in range(PIECES)]
        length, src_len = sk.shape[2], ck.shape[2]
        row_bf16, row_f32 = pltpu.VMEM((rows, width), bf16), pltpu.VMEM((rows, width), f32)
        full = pltpu.VMEM((n * cols, width), bf16)
        columns = pltpu.VMEM((rows // UPDATE, width, LANES), bf16)
        ln_row = pltpu.VMEM((1, width), f32)
        index = pltpu.SMEM((rows,), i32)
        exchange = pltpu.VMEM((n, 3, rows, cols), bf16)
        operands = (hidden, positions, expert_idx, enc_mask, ln_self, ln_cross, ln_ffn, rel_bias, w_router.T,
                    wq_self.T, wk_self.T, wv_self.T, wo_self.T, wq_cross.T, wo_cross.T, sk, sv, ck, cv)
        gathered = pl.pallas_call(
            functools.partial(gather_kernel, n, head_dim),
            out_shape=(row_bf16, pltpu.VMEM((n, rows, width), bf16),
                       pltpu.VMEM((n, rows, LANES), i32), pltpu.VMEM((n, 1, width), f32),
                       columns, columns, *pieces),
            in_specs=[HBM] * len(operands),
            out_specs=(VMEM,) * (6 + len(pieces)),
            scratch_shapes=[pltpu.VMEM(ck.shape, bf16), pltpu.VMEM((rows // PIECES,) + cv.shape[1:], bf16), full, full, full,
                            row_bf16, index, index, pltpu.VMEM(enc_mask.shape, i32), ln_row, ln_row, ln_row,
                            pltpu.VMEM(rel_bias.shape, f32), pltpu.VMEM((n, rows, width), bf16),
                            pltpu.VMEM((3, cols, width), bf16), exchange, exchange, row_f32, pltpu.VMEM((2, rows, width), f32),
                            pltpu.VMEM((rows, pad_heads, length), f32), pltpu.VMEM((rows, pad_heads, length), bf16),
                            pltpu.VMEM((rows, pad_heads, LANES), f32), row_f32,
                            dma((20 + 2 * PIECES,)), dma((5,)), dma((5,)), dma((3,)), dma((4, 3)), dma((3,))],
            compiler_params=pltpu.CompilerParams(collective_id=0, has_side_effects=True, vmem_limit_bytes=40 << 19),
            name='gather')(*(hbm(x) for x in operands))
        h2, xall, eid_all, wr_all, kt, vt, *caches = gathered

        part, gate, new_k, new_v, *_ = pl.pallas_call(
            functools.partial(update_kernel, n, capacity),
            out_shape=(pltpu.VMEM((n, rows, width), f32), pltpu.VMEM((rows, LANES), f32),
                       pltpu.HBM(sk.shape, bf16), pltpu.HBM(sv.shape, bf16), *pieces),
            in_specs=[SMEM] + [VMEM] * (7 + len(pieces)),
            out_specs=(VMEM, VMEM, HBM, HBM) + (VMEM,) * len(pieces),
            input_output_aliases={8 + t: 4 + t for t in range(len(pieces))},
            scratch_shapes=[pltpu.VMEM((group_rows, experts * units), bf16), dma((2,))],
            compiler_params=pltpu.CompilerParams(vmem_limit_bytes=10 << 19),
            name='attend')(positions, kt, vt, xall, eid_all, wr_all, w_in, w_out, *caches)

        hidden_out = pl.pallas_call(
            functools.partial(reduce_kernel, n),
            out_shape=jax.ShapeDtypeStruct((rows, width), bf16),
            in_specs=[VMEM] * 3,
            out_specs=VMEM,
            scratch_shapes=[pltpu.VMEM((n, rows, width), f32), dma, dma],
            compiler_params=pltpu.CompilerParams(collective_id=1, has_side_effects=True, vmem_limit_bytes=4 << 20),
            name='experts')(part, gate, h2)

        def unflat(cache):
            return cache.reshape(rows, heads, head_dim, cache.shape[2]).transpose(0, 1, 3, 2)

        return hidden_out, unflat(new_k), unflat(new_v)

    return jax.shard_map(decoder_block, mesh=mesh, in_specs=in_specs, out_specs=out_specs, check_vma=False)
```

time: 593 us -> 54 us (0.09)
  waiting for transfers between devices: 255 us -> 0 us
  local copies, waits for them, and re-layouts: 178 us -> 0.62 us
  matrix products: 84.2 us -> 0 us
  Pallas kernels: 0 us -> 52.5 us
  blocking collectives: 36.8 us -> 0 us
  other arithmetic: 22.8 us -> 0 us
  between operations: 14.6 us -> 0.71 us
    all_gather x8 -> x0, waiting for transfers between devices: 250 us -> none  [the longest x1 170 us: decoder_block(): win_full = gather_ws(w_in, axis=2)]
    gather x9 -> x0, local copies, waits for them, and re-layouts: 166 us -> none  [the longest x4 69.3 us: decoder_block(): jnp.take(wout_full, expert_idx, axis=0)]
    dot_general x13 -> x0, matrix products: 84.2 us -> none  [the longest x1 27.4 us: decoder_block(): jnp.einsum('bd,bdf->bf', x_norm, jnp.take(win_full, expert_idx, axis=0),...]
    pallas_call x0 -> x3, Pallas kernels: none -> 52.5 us  [the longest x1 35.5 us: decoder_block(): pl.pallas_call(functools.partial(gather_kernel, n, head_dim), out_shape=(...]
    unnamed x1 -> x0, blocking collectives: 25 us -> none
    select_n x4 -> x0, other arithmetic: 15 us -> none  [the longest x1 14.4 us: decoder_block(): new_self_v = jnp.where(write_mask, v_new[:, :, None, :], self_v)]
    all_gather x1 -> x0, blocking collectives: 11.8 us -> none  [decoder_block(): router_full = gather_ws(w_router, axis=1)]
  transfers between devices with their start and end apart: 8 -> 0, of which waited for: 2 -> 0; matrix products, arithmetic and copies ran while one was open for 31% -> 0% of each run, Pallas kernels for 0% -> 0%
where the time goes in v3:
time: 54 us; the launch traced here: 53.9 us
  Pallas kernels  52.5 us (97%)
  between operations  0.71 us (1%)
  local copies, waits for them, and re-layouts  0.62 us (1%)
    pallas_call x1, Pallas kernels, decoder_block(): pl.pallas_call(functools.partial(gather_kernel, n, head_dim), out_shape=(...  35.5 us
    pallas_call x1, Pallas kernels, decoder_block(): pl.pallas_call(functools.partial(update_kernel, n, capacity), out_shape=(...  9.7 us
    pallas_call x1, Pallas kernels, decoder_block(): pl.pallas_call(functools.partial(reduce_kernel, n), out_shape=jax.ShapeDt...  7.34 us

profile of v3, /device:TPU:0, one launch (start us, length us, event | category | flops | bytes accessed | tf_op | source)
XLA Modules:
  0.0 53.9 jit_solution(7794741656118015703)
XLA Ops:
  0.6 0.0 copy-start
  0.6 0.0 copy-start.1
  0.7 0.0 copy-start.2
  0.7 35.5 %gather.1 = (bf16[16,768]{1,0:T(8,128)(2,1)S(1)}, bf16[8,16,768]{2,1,0:T(8,128)(2,1)S(1)}, s32[8,16,128]{2,1,0:T(8,128)S(1)}, f32[8,1,768]{2,1,0:T(1,128)S(1)}, ...) custom-call(bf16[16,768]{1,0:T(8,128)(2,1)} %hid.1, ...), custom_call_target="tpu_custom_call" | custom-call | tf_op jit(solution)/shard_map/gather/pallas_call | solution.py:405
  36.2 0.0 copy-done
  36.2 0.0 copy-done.1
  36.2 0.0 copy-done.2
  36.2 9.7 %attend.1 = (f32[8,16,768]{2,1,0:T(8,128)S(1)}, f32[16,128]{1,0:T(8,128)S(1)}, bf16[16,768,512]{2,1,0:T(8,128)(2,1)}, bf16[16,768,512]{2,1,0:T(8,128)(2,1)}, bf1...) custom-call(s32[16]{0:T(128)S(1)} %copy-done.2, ...), custom_call_target="tpu_custom_call", output_to_operand_aliasing={{4}: (8, {}), {5}: (9, {}), {6}: (10, {}), {7}: (11, {})} | custom-call | tf_op jit(solution)/shard_map/attend/pallas_call | solution.py:423
  45.9 7.3 %experts.1 = bf16[16,768]{1,0:T(8,128)(2,1)S(1)} custom-call(f32[8,16,768]{2,1,0:T(8,128)S(1)} %get-tuple-element.26.part, f32[16,128]{1,0:T(8,128)S(1)} %get-tuple-element.27.gate, bf16[16,768]{1,0:T(8,128)(2,1)S(1)} %get-tuple-element.28.h2), custom_call_target="tpu_custom_call" | custom-call | tf_op jit(solution)/shard_map/experts/pallas_call | solution.py:434
  53.3 0.6 %copy.33 = bf16[16,768]{1,0:T(8,128)(2,1)} copy(bf16[16,768]{1,0:T(8,128)(2,1)S(1)} %experts.1) | data formatting | bytes 49152
Async XLA Ops:
  0.6 35.5 %copy-start = (bf16[8,768,384]{2,1,0:T(8,128)(2,1)S(1)}, bf16[8,768,384]{2,1,0:T(8,128)(2,1)}, u32[]{:S(2)}) copy-start(bf16[8,768,384]{2,1,0:T(8,128)(2,1)} %win.1) | copy-start | bytes 14155780
  0.6 35.5 %copy-start.1 = (bf16[8,384,768]{2,1,0:T(8,128)(2,1)S(1)}, bf16[8,384,768]{2,1,0:T(8,128)(2,1)}, u32[]{:S(2)}) copy-start(bf16[8,384,768]{2,1,0:T(8,128)(2,1)} %wout.1) | copy-start | bytes 14155780
  0.7 35.5 %copy-start.2 = (s32[16]{0:T(128)S(1)}, s32[16]{0:T(128)}, u32[]{:S(2)}) copy-start(s32[16]{0:T(128)} %pos.3) | copy-start | bytes 196

commit v4 on v3

--- a/solution.py
+++ b/solution.py
@@ -34,6 +34,14 @@
     for k in range(1, n):
         pl.semaphore_signal(barrier, inc=1, device_id={'ws': lax.rem(me + k, n)}, device_id_type=MESH)
     pl.semaphore_wait(barrier, n - 1)
+
+
+def neighbours(me):
+    core, xpos, ypos = lax.rem(me, 2), lax.rem(me // 2, 2), me // 4
+    other, across_x, across_y = 1 - 2 * core, 2 - 4 * xpos, 4 - 8 * ypos
+    xnb, ynb, diag = me + across_x, me + across_y, me + across_x + across_y
+    far_first = [diag, diag + other, xnb, ynb, xnb + other, ynb + other, me + other]
+    return me + other, xnb, ynb, diag, far_first
 
 
 def remote(src, dst, send_sem, recv_sem, peer):
@@ -73,12 +81,7 @@
     src_len = ck.shape[2]
     piece = rows // PIECES
     f32, bf16 = jnp.float32, jnp.bfloat16
-    core, xpos, ypos = lax.rem(me, 2), lax.rem(me // 2, 2), me // 4
-    pair = me + 1 - 2 * core
-    xnb = me + 2 - 4 * xpos
-    ynb = me + 4 - 8 * ypos
-    diag = me + 2 - 4 * xpos + 4 - 8 * ypos
-    peers = [lax.rem(me + k, n) for k in range(1, n)]
+    pair, xnb, ynb, diag, peers = neighbours(me)
 
     count = []
 
@@ -116,17 +119,14 @@
             c.start()
         own_copies.append(local(src, at))
 
-    own_share(0)
     load_self = [local(src.at[pl.ds(t * piece, piece)], self_kv[i * PIECES + t])
                  for i, src in enumerate((sk, sv)) for t in range(PIECES)]
     load_cross = [local(ck, ck_v), local(cv.at[pl.ds(0, piece)], cv_v)]
     hall[me] = hid_v[...]
     for r in range(rows):
         eid_all[me, r:r + 1, :] = jnp.full((1, LANES), eid_s[r], jnp.int32)
-    for p in peers:
-        remote(eid_all.at[me], eid_all.at[me], send.at[1], recv.at[1], p).start()
-        remote(wr_all.at[me], wr_all.at[me], send.at[2], recv.at[2], p).start()
-
+
+    own_share(0)
     key_pos = lax.broadcasted_iota(jnp.int32, (1, length), 1)
     table = reverse_lanes(jnp.concatenate(
         [bias_v[...], jnp.zeros((heads - bias_v.shape[0], length), f32)], axis=0))
@@ -181,7 +181,7 @@
         own_copies[i].wait()
 
     all_of(qkv, 3).wait_recv()
-    for c in load_self:
+    for c in load_self[:PIECES]:
         c.wait()
 
     def assemble(i):
@@ -235,10 +235,15 @@
     relay(1)
     self_softmax()
     relay_diag(0)
+    for c in load_self[PIECES:]:
+        c.wait()
     self_context(0)
     self_context(1)
     relay_diag(1)
     relay(2)
+    for p in peers:
+        remote(eid_all.at[me], eid_all.at[me], send.at[1], recv.at[1], p).start()
+        remote(wr_all.at[me], wr_all.at[me], send.at[2], recv.at[2], p).start()
 
     wait_weight(0)
     h1 = (hid_v[...].astype(f32) + project(ctx_sc[...].astype(bf16), wo_all[...])).astype(bf16)
@@ -262,10 +267,10 @@
         store_context(b, project(p_sc[b, :, 0:src_len], ck_v[r]))
 
     over_rows(0, piece, cross_scores)
-    relay_diag(2)
     load_late = local(cv.at[pl.ds(piece, piece)], ck_v.at[pl.ds(0, piece)])
     over_rows(piece, rows, cross_scores)
     over_rows(0, rows, cross_softmax)
+    relay_diag(2)
     over_rows(0, piece, cross_context)
     load_late.wait()
     over_rows(piece, rows, cross_context_late)
@@ -307,6 +312,12 @@
         @pl.loop(0, piece // UPDATE)
         def _(i):
             g = t * (piece // UPDATE) + i
+            def write(j):
+                r = i * UPDATE + j
+                b = t * piece + r
+                pltpu.make_async_copy(keys.at[r], nk.at[b], out_sem.at[0]).start()
+                pltpu.make_async_copy(vals.at[r], nv.at[b], out_sem.at[1]).start()
+
             for j in range(UPDATE):
                 r = i * UPDATE + j
                 b = t * piece + r
@@ -315,11 +326,9 @@
                 hit = lane == p % LANES
                 for cache, new in ((keys, kt), (vals, vt)):
                     cache[r, :, win_at] = jnp.where(hit, new[g, :, j:j + 1], cache[r, :, win_at])
-            for j in range(UPDATE):
-                r = i * UPDATE + j
-                b = t * piece + r
-                pltpu.make_async_copy(keys.at[r], nk.at[b], out_sem.at[0]).start()
-                pltpu.make_async_copy(vals.at[r], nv.at[b], out_sem.at[1]).start()
+                if j:
+                    write(j - 1)
+            write(UPDATE - 1)
 
     eid = eid_all[...].reshape(group_rows, LANES)
     eid_col = eid[:, 0:1]
@@ -351,8 +360,7 @@
     me = lax.axis_index('ws')
     f32 = jnp.float32
     entry_barrier(me, n)
-    for k in range(1, n):
-        peer = lax.rem(me + k, n)
+    for peer in neighbours(me)[-1]:
         remote(part.at[peer], acc.at[me], send, recv, peer).start()
     acc[me] = part[me]
     others = pl.ds(0, n - 1)

time: 54 us -> 52 us (0.963)
  Pallas kernels: 52.5 us -> 50.6 us
    pallas_call x1, Pallas kernels: 35.5 us -> 34.2 us  [decoder_block(): pl.pallas_call(functools.partial(gather_kernel, n, head_dim), out_shape=(...]
where the time goes in v4:
time: 52 us; the launch traced here: 51.9 us
  Pallas kernels  50.6 us (97%)
  between operations  0.71 us (1%)
  local copies, waits for them, and re-layouts  0.62 us (1%)
    pallas_call x1, Pallas kernels, decoder_block(): pl.pallas_call(functools.partial(gather_kernel, n, head_dim), out_shape=(...  34.2 us
    pallas_call x1, Pallas kernels, decoder_block(): pl.pallas_call(functools.partial(update_kernel, n, capacity), out_shape=(...  9.29 us
    pallas_call x1, Pallas kernels, decoder_block(): pl.pallas_call(functools.partial(reduce_kernel, n), out_shape=jax.ShapeDt...  7.04 us

profile of v4, /device:TPU:0, one launch (start us, length us, event | category | flops | bytes accessed | tf_op | source)
XLA Modules:
  0.0 51.9 jit_solution(15118011472805221236)
XLA Ops:
  0.6 0.0 copy-start
  0.6 0.0 copy-start.1
  0.7 0.0 copy-start.2
  0.7 34.2 %gather.1 = (bf16[16,768]{1,0:T(8,128)(2,1)S(1)}, bf16[8,16,768]{2,1,0:T(8,128)(2,1)S(1)}, s32[8,16,128]{2,1,0:T(8,128)S(1)}, f32[8,1,768]{2,1,0:T(1,128)S(1)}, ...) custom-call(bf16[16,768]{1,0:T(8,128)(2,1)} %hid.1, ...), custom_call_target="tpu_custom_call" | custom-call | tf_op jit(solution)/shard_map/gather/pallas_call | solution.py:413
  34.9 0.0 copy-done
  34.9 0.0 copy-done.1
  34.9 0.0 copy-done.2
  34.9 9.3 %attend.1 = (f32[8,16,768]{2,1,0:T(8,128)S(1)}, f32[16,128]{1,0:T(8,128)S(1)}, bf16[16,768,512]{2,1,0:T(8,128)(2,1)}, bf16[16,768,512]{2,1,0:T(8,128)(2,1)}, bf1...) custom-call(s32[16]{0:T(128)S(1)} %copy-done.2, ...), custom_call_target="tpu_custom_call", output_to_operand_aliasing={{4}: (8, {}), {5}: (9, {}), {6}: (10, {}), {7}: (11, {})} | custom-call | tf_op jit(solution)/shard_map/attend/pallas_call | solution.py:431
  44.2 7.0 %experts.1 = bf16[16,768]{1,0:T(8,128)(2,1)S(1)} custom-call(f32[8,16,768]{2,1,0:T(8,128)S(1)} %get-tuple-element.26.part, f32[16,128]{1,0:T(8,128)S(1)} %get-tuple-element.27.gate, bf16[16,768]{1,0:T(8,128)(2,1)S(1)} %get-tuple-element.28.h2), custom_call_target="tpu_custom_call" | custom-call | tf_op jit(solution)/shard_map/experts/pallas_call | solution.py:442
  51.3 0.6 %copy.33 = bf16[16,768]{1,0:T(8,128)(2,1)} copy(bf16[16,768]{1,0:T(8,128)(2,1)S(1)} %experts.1) | data formatting | bytes 49152
Async XLA Ops:
  0.6 34.3 %copy-start = (bf16[8,768,384]{2,1,0:T(8,128)(2,1)S(1)}, bf16[8,768,384]{2,1,0:T(8,128)(2,1)}, u32[]{:S(2)}) copy-start(bf16[8,768,384]{2,1,0:T(8,128)(2,1)} %win.1) | copy-start | bytes 14155780
  0.6 34.3 %copy-start.1 = (bf16[8,384,768]{2,1,0:T(8,128)(2,1)S(1)}, bf16[8,384,768]{2,1,0:T(8,128)(2,1)}, u32[]{:S(2)}) copy-start(bf16[8,384,768]{2,1,0:T(8,128)(2,1)} %wout.1) | copy-start | bytes 14155780
  0.7 34.3 %copy-start.2 = (s32[16]{0:T(128)S(1)}, s32[16]{0:T(128)}, u32[]{:S(2)}) copy-start(s32[16]{0:T(128)} %pos.3) | copy-start | bytes 196

commit v5 on v4

--- a/solution.py
+++ b/solution.py
@@ -10,7 +10,11 @@
 NEG_BIG = -1e30
 LANES = 128
 GROUP = 4
+SOFTMAX_GROUP = 8
+BIAS_GROUP = 4
+MXU_HEADS = 6
 UPDATE = 4
+READY = 4
 PIECES = 2
 NT = (((1,), (1,)), ((), ()))
 MESH = pl.DeviceIdType.MESH
@@ -73,7 +77,7 @@
                   h2_out, xall, eid_all, wr_all, *rest):
     (kt_out, vt_out), self_kv = rest[:2], rest[2:2 * PIECES + 2]
     (ck_v, cv_v, wo_all, wqc_all, woc_all, hid_v, pos_s, eid_s, mask_v, ln_sv, ln_cv, ln_fv, bias_v, hall, wqkv, snd, qkv,
-     q_sc, kv_out, s_sc, p_sc, pn_sc, ctx_sc, loc_sem, send, recv, sw, rw, rp) = rest[2 * PIECES + 2:]
+     q_sc, kv_out, s_sc, p_sc, pn_sc, ctx_sc, col_sc, loc_sem, send, recv, sw, rw, rp) = rest[2 * PIECES + 2:]
     me = lax.axis_index('ws')
     rows, width = hid.shape
     cols = wq.shape[0]
@@ -108,21 +112,29 @@
 
     fulls = ((wo, wo_all), (wqc, wqc_all), (woc, woc_all))
     half = cols // 2
-    to_x, to_y, own_copies = [], [], []
+    own_copies = []
+    moves = {}
+
+    def move(name, i, src_dev, lo, size, sem, peer, src=None):
+        dst = fulls[i][1].at[pl.ds(pl.multiple_of(src_dev * cols + lo, half), size)]
+        moves[name, i] = remote(dst if src is None else src, dst, sw.at[i], sem, peer)
+        moves[name, i].start()
 
     def own_share(i):
         src, dst = fulls[i]
-        at = dst.at[pl.ds(pl.multiple_of(me * cols, cols), cols)]
-        to_x.append(remote(src, at, sw.at[i], rw.at[0, i], xnb))
-        to_y.append(remote(src, at, sw.at[i], rw.at[1, i], ynb))
-        for c in (to_x[-1], to_y[-1], remote(src, at, sw.at[i], rp.at[i], pair)):
-            c.start()
-        own_copies.append(local(src, at))
+        upper, lower = src.at[pl.ds(0, half)], src.at[pl.ds(half, half)]
+        move('x0', i, me, 0, half, rw.at[0, i], xnb, upper)
+        move('y1', i, me, half, half, rw.at[1, i], ynb, lower)
+        move('x1', i, me, half, half, rw.at[2, i], xnb, lower)
+        move('y0', i, me, 0, half, rw.at[3, i], ynb, upper)
+        move('pair', i, me, 0, cols, rp.at[i], pair, src)
+        own_copies.append(local(src, dst.at[pl.ds(pl.multiple_of(me * cols, cols), cols)]))
 
     load_self = [local(src.at[pl.ds(t * piece, piece)], self_kv[i * PIECES + t])
                  for i, src in enumerate((sk, sv)) for t in range(PIECES)]
     load_cross = [local(ck, ck_v), local(cv.at[pl.ds(0, piece)], cv_v)]
     hall[me] = hid_v[...]
+    col_sc[...] = jnp.zeros_like(col_sc)
     for r in range(rows):
         eid_all[me, r:r + 1, :] = jnp.full((1, LANES), eid_s[r], jnp.int32)
 
@@ -131,15 +143,15 @@
     table = reverse_lanes(jnp.concatenate(
         [bias_v[...], jnp.zeros((heads - bias_v.shape[0], length), f32)], axis=0))
 
-    @pl.loop(0, rows // GROUP)
+    @pl.loop(0, rows // BIAS_GROUP)
     def _(i):
-        marks = [jnp.full((1, length), pos_s[i * GROUP + j], jnp.int32) for j in range(GROUP)]
-        turned, step = [table] * GROUP, 1
+        marks = [jnp.full((1, length), pos_s[i * BIAS_GROUP + j], jnp.int32) for j in range(BIAS_GROUP)]
+        turned, step = [table] * BIAS_GROUP, 1
         while step < length:
             turned = [jnp.where(((p + 1) & step) != 0, pltpu.roll(t, step, 1), t) for p, t in zip(marks, turned)]
             step *= 2
-        for j in range(GROUP):
-            s_sc[i * GROUP + j] = jnp.where(key_pos <= marks[j], turned[j], NEG_BIG)
+        for j in range(BIAS_GROUP):
+            s_sc[i * BIAS_GROUP + j] = jnp.where(key_pos <= marks[j], turned[j], NEG_BIG)
 
     all_of(hall, 0).wait_recv()
     for c in proj:
@@ -153,27 +165,25 @@
     qkv[me] = snd[me]
     own_share(1)
 
-    def forward(src_dev, lo, size, i, sem, peer):
-        dst = fulls[i][1].at[pl.ds(pl.multiple_of(src_dev * cols + lo, half), size)]
-        c = remote(dst, dst, sw.at[i], sem, peer)
-        c.start()
-        return c
-
-    relay_y, relay_x = {}, {}
-
     def relay(i):
-        to_x[i].wait_recv()
-        relay_y[i] = forward(xnb, 0, half, i, rw.at[2, i], ynb)
-        forward(xnb, 0, cols, i, rp.at[i], pair)
-        to_y[i].wait_recv()
-        relay_x[i] = forward(ynb, half, half, i, rw.at[3, i], xnb)
-        forward(ynb, 0, cols, i, rp.at[i], pair)
+        moves['x0', i].wait_recv()
+        move('ry', i, xnb, 0, half, rw.at[4, i], ynb)
+        moves['y1', i].wait_recv()
+        move('rx', i, ynb, half, half, rw.at[5, i], xnb)
+        move('p0', i, xnb, 0, half, rp.at[i], pair)
+        move('p1', i, ynb, half, half, rp.at[i], pair)
+
+    def relay_rest(i):
+        moves['x1', i].wait_recv()
+        move('p2', i, xnb, half, half, rp.at[i], pair)
+        moves['y0', i].wait_recv()
+        move('p3', i, ynb, 0, half, rp.at[i], pair)
 
     def relay_diag(i):
-        relay_y[i].wait_recv()
-        forward(diag, 0, half, i, rp.at[i], pair)
-        relay_x[i].wait_recv()
-        forward(diag, half, half, i, rp.at[i], pair)
+        moves['ry', i].wait_recv()
+        move('p4', i, diag, 0, half, rp.at[i], pair)
+        moves['rx', i].wait_recv()
+        move('p5', i, diag, half, half, rp.at[i], pair)
 
     def wait_weight(i):
         theirs = fulls[i][1].at[pl.ds(0, 4 * cols)]
@@ -192,18 +202,35 @@
     kv_out[1] = assemble(2)
     head_mask = head_mask_of(heads, width, head_dim)
 
-    def over_rows(lo, hi, body):
-        @pl.loop(0, (hi - lo) // GROUP)
+    def over_rows(lo, hi, body, group=GROUP):
+        @pl.loop(0, (hi - lo) // group)
         def _(i):
-            for j in range(GROUP):
-                body(lo + i * GROUP + j, i * GROUP + j)
+            for j in range(group):
+                body(lo + i * group + j, i * group + j)
 
     def softmax(s):
         e = jnp.exp(s - jnp.max(s, axis=-1, keepdims=True))
         return (e / jnp.sum(e, axis=-1, keepdims=True)).astype(bf16)
 
-    def store_context(b, o):
+    split = MXU_HEADS * head_dim
+    lane = lax.broadcasted_iota(jnp.int32, (1, LANES), 1)
+
+    def store_context(b, probs, vals, r, new=0.0):
+        size = probs.shape[1]
+        o = jnp.concatenate([project(probs, vals[r, 0:split]), jnp.zeros((heads, width - split), f32)], axis=1) + new
         ctx_sc[pl.ds(b, 1), :] = jnp.sum(jnp.where(head_mask, o, 0.0), axis=0, keepdims=True)
+        weights = probs.astype(f32)
+        for lo in range(split, width, head_dim):
+            h = lo // head_dim
+            terms = vals[r, lo:lo + head_dim].astype(f32) * weights[h:h + 1]
+            folded = functools.reduce(jnp.add, [terms[:, c:c + LANES] for c in range(0, size, LANES)])
+            column = jnp.sum(folded, axis=1, keepdims=True)
+            at = slice(lo - split, lo - split + head_dim)
+            col_sc[at] = jnp.where(lane == b, column, col_sc[at])
+
+    def contexts():
+        late = col_sc[...].T[0:rows]
+        return (ctx_sc[...] + jnp.concatenate([jnp.zeros((rows, split), f32), late], axis=1)).astype(bf16)
 
     def self_scores(t):
         def body(b, r):
@@ -220,33 +247,34 @@
             p_new = jnp.sum(jnp.where(hit, probs, 0.0), axis=1, keepdims=True)
             pn_sc[b] = jnp.broadcast_to(p_new, (heads, LANES))
             p_sc[b] = jnp.where(hit, 0.0, probs).astype(bf16)
-        over_rows(0, rows, body)
+        over_rows(0, rows, body, SOFTMAX_GROUP)
 
     def self_context(t):
         def body(b, r):
-            o = project(p_sc[b], self_kv[PIECES + t][r])
-            store_context(b, o + pn_sc[b, :, 0:1] * kv_out[1, pl.ds(b, 1), :])
+            store_context(b, p_sc[b], self_kv[PIECES + t], r, pn_sc[b, :, 0:1] * kv_out[1, pl.ds(b, 1), :])
         over_rows(t * piece, (t + 1) * piece, body)
 
     relay(0)
+    self_scores(0)
+    relay(1)
     own_share(2)
-    self_scores(0)
     self_scores(1)
-    relay(1)
+    relay_rest(0)
     self_softmax()
-    relay_diag(0)
     for c in load_self[PIECES:]:
         c.wait()
     self_context(0)
+    relay_diag(0)
+    relay_rest(1)
     self_context(1)
     relay_diag(1)
+    wait_weight(0)
+    h1 = (hid_v[...].astype(f32) + project(contexts(), wo_all[...])).astype(bf16)
     relay(2)
     for p in peers:
         remote(eid_all.at[me], eid_all.at[me], send.at[1], recv.at[1], p).start()
         remote(wr_all.at[me], wr_all.at[me], send.at[2], recv.at[2], p).start()
 
-    wait_weight(0)
-    h1 = (hid_v[...].astype(f32) + project(ctx_sc[...].astype(bf16), wo_all[...])).astype(bf16)
     wait_weight(1)
     q_sc[...] = project(rms_norm(h1, ln_cv[...]), wqc_all[...]).astype(bf16).astype(f32)
     for c in load_cross:
@@ -261,21 +289,22 @@
         p_sc[b, :, 0:src_len] = softmax(s_sc[b, :, 0:src_len])
 
     def cross_context(b, r):
-        store_context(b, project(p_sc[b, :, 0:src_len], cv_v[b]))
+        store_context(b, p_sc[b, :, 0:src_len], cv_v, b)
 
     def cross_context_late(b, r):
-        store_context(b, project(p_sc[b, :, 0:src_len], ck_v[r]))
+        store_context(b, p_sc[b, :, 0:src_len], ck_v, r)
 
     over_rows(0, piece, cross_scores)
     load_late = local(cv.at[pl.ds(piece, piece)], ck_v.at[pl.ds(0, piece)])
     over_rows(piece, rows, cross_scores)
-    over_rows(0, rows, cross_softmax)
+    relay_rest(2)
+    over_rows(0, rows, cross_softmax, SOFTMAX_GROUP)
     relay_diag(2)
     over_rows(0, piece, cross_context)
     load_late.wait()
     over_rows(piece, rows, cross_context_late)
     wait_weight(2)
-    h2 = (h1.astype(f32) + project(ctx_sc[...].astype(bf16), woc_all[...])).astype(bf16)
+    h2 = (h1.astype(f32) + project(contexts(), woc_all[...])).astype(bf16)
     xall[me] = rms_norm(h2, ln_fv[...])
     h2_out[...] = h2
     third = [remote(xall.at[me], xall.at[me], send.at[4], recv.at[4], p) for p in peers]
@@ -286,6 +315,11 @@
         for g in range(rows // UPDATE):
             shifted = cols_t if g == 0 else pltpu.roll(cols_t, LANES - g * UPDATE, 1)
             ref[g] = shifted.astype(bf16)
+    for j in range(READY):
+        hit = key_pos == pos_s[j]
+        for i, ref in enumerate((kt_out, vt_out)):
+            cache = self_kv[i * PIECES]
+            cache[j] = jnp.where(hit, ref[0, :, j:j + 1], cache[j])
     for i, ref in ((1, eid_all), (2, wr_all), (4, xall)):
         all_of(ref, i).wait_recv()
     for i, ref in enumerate((hall, eid_all, wr_all, snd, xall)):
@@ -306,10 +340,14 @@
     f32 = jnp.float32
     lane = lax.broadcasted_iota(jnp.int32, (1, LANES), 1)
 
+    for b in range(READY):
+        pltpu.make_async_copy(self_kv[0].at[b], nk.at[b], out_sem.at[0]).start()
+        pltpu.make_async_copy(self_kv[PIECES].at[b], nv.at[b], out_sem.at[1]).start()
+
     for t in range(PIECES):
         keys, vals = self_kv[t], self_kv[PIECES + t]
 
-        @pl.loop(0, piece // UPDATE)
+        @pl.loop(READY // UPDATE if t == 0 else 0, piece // UPDATE)
         def _(i):
             g = t * (piece // UPDATE) + i
             def write(j):
@@ -423,7 +461,8 @@
                             pltpu.VMEM((3, cols, width), bf16), exchange, exchange, row_f32, pltpu.VMEM((2, rows, width), f32),
                             pltpu.VMEM((rows, pad_heads, length), f32), pltpu.VMEM((rows, pad_heads, length), bf16),
                             pltpu.VMEM((rows, pad_heads, LANES), f32), row_f32,
-                            dma((20 + 2 * PIECES,)), dma((5,)), dma((5,)), dma((3,)), dma((4, 3)), dma((3,))],
+                            pltpu.VMEM((width - MXU_HEADS * head_dim, LANES), f32),
+                            dma((20 + 2 * PIECES,)), dma((5,)), dma((5,)), dma((3,)), dma((6, 3)), dma((3,))],
             compiler_params=pltpu.CompilerParams(collective_id=0, has_side_effects=True, vmem_limit_bytes=40 << 19),
             name='gather')(*(hbm(x) for x in operands))
         h2, xall, eid_all, wr_all, kt, vt, *caches = gathered

time: 52 us -> 48.5 us (0.933)
  Pallas kernels: 50.6 us -> 47.1 us
    pallas_call x1, Pallas kernels: 34.2 us -> 30.8 us  [decoder_block(): pl.pallas_call(functools.partial(gather_kernel, n, head_dim), out_shape=(...]
where the time goes in v5:
time: 48.5 us; the launch traced here: 48.4 us
  Pallas kernels  47.1 us (97%)
  between operations  0.71 us (1%)
  local copies, waits for them, and re-layouts  0.62 us (1%)
    pallas_call x1, Pallas kernels, decoder_block(): pl.pallas_call(functools.partial(gather_kernel, n, head_dim), out_shape=(...  30.8 us
    pallas_call x1, Pallas kernels, decoder_block(): pl.pallas_call(functools.partial(update_kernel, n, capacity), out_shape=(...  8.91 us
    pallas_call x1, Pallas kernels, decoder_block(): pl.pallas_call(functools.partial(reduce_kernel, n), out_shape=jax.ShapeDt...  7.35 us

profile of v5, /device:TPU:0, one launch (start us, length us, event | category | flops | bytes accessed | tf_op | source)
XLA Modules:
  0.0 48.4 jit_solution(5227716440570803613)
XLA Ops:
  0.6 0.0 copy-start
  0.6 0.0 copy-start.1
  0.7 0.0 copy-start.2
  0.7 30.8 %gather.1 = (bf16[16,768]{1,0:T(8,128)(2,1)S(1)}, bf16[8,16,768]{2,1,0:T(8,128)(2,1)S(1)}, s32[8,16,128]{2,1,0:T(8,128)S(1)}, f32[8,1,768]{2,1,0:T(1,128)S(1)}, ...) custom-call(bf16[16,768]{1,0:T(8,128)(2,1)} %hid.1, ...), custom_call_target="tpu_custom_call" | custom-call | tf_op jit(solution)/shard_map/gather/pallas_call | solution.py:451
  31.5 0.0 copy-done
  31.5 0.0 copy-done.1
  31.5 0.0 copy-done.2
  31.5 8.9 %attend.1 = (f32[8,16,768]{2,1,0:T(8,128)S(1)}, f32[16,128]{1,0:T(8,128)S(1)}, bf16[16,768,512]{2,1,0:T(8,128)(2,1)}, bf16[16,768,512]{2,1,0:T(8,128)(2,1)}, bf1...) custom-call(s32[16]{0:T(128)S(1)} %copy-done.2, ...), custom_call_target="tpu_custom_call", output_to_operand_aliasing={{4}: (8, {}), {5}: (9, {}), {6}: (10, {}), {7}: (11, {})} | custom-call | tf_op jit(solution)/shard_map/attend/pallas_call | solution.py:470
  40.4 7.3 %experts.1 = bf16[16,768]{1,0:T(8,128)(2,1)S(1)} custom-call(f32[8,16,768]{2,1,0:T(8,128)S(1)} %get-tuple-element.26.part, f32[16,128]{1,0:T(8,128)S(1)} %get-tuple-element.27.gate, bf16[16,768]{1,0:T(8,128)(2,1)S(1)} %get-tuple-element.28.h2), custom_call_target="tpu_custom_call" | custom-call | tf_op jit(solution)/shard_map/experts/pallas_call | solution.py:481
  47.8 0.6 %copy.33 = bf16[16,768]{1,0:T(8,128)(2,1)} copy(bf16[16,768]{1,0:T(8,128)(2,1)S(1)} %experts.1) | data formatting | bytes 49152
Async XLA Ops:
  0.6 30.9 %copy-start = (bf16[8,768,384]{2,1,0:T(8,128)(2,1)S(1)}, bf16[8,768,384]{2,1,0:T(8,128)(2,1)}, u32[]{:S(2)}) copy-start(bf16[8,768,384]{2,1,0:T(8,128)(2,1)} %win.1) | copy-start | bytes 14155780
  0.6 30.9 %copy-start.1 = (bf16[8,384,768]{2,1,0:T(8,128)(2,1)S(1)}, bf16[8,384,768]{2,1,0:T(8,128)(2,1)}, u32[]{:S(2)}) copy-start(bf16[8,384,768]{2,1,0:T(8,128)(2,1)} %wout.1) | copy-start | bytes 14155780
  0.7 30.9 %copy-start.2 = (s32[16]{0:T(128)S(1)}, s32[16]{0:T(128)}, u32[]{:S(2)}) copy-start(s32[16]{0:T(128)} %pos.3) | copy-start | bytes 196

commit v6 on v5

--- a/solution.py
+++ b/solution.py
@@ -394,19 +394,28 @@
         pltpu.make_async_copy(ref, ref, out_sem.at[i]).wait()
 
 
-def reduce_kernel(n, part, gate, h2, out, acc, send, recv):
+def reduce_kernel(n, part, gate, h2, out, near, mixed, far, s1, r1, s2, r2):
     me = lax.axis_index('ws')
     f32 = jnp.float32
     entry_barrier(me, n)
-    for peer in neighbours(me)[-1]:
-        remote(part.at[peer], acc.at[me], send, recv, peer).start()
-    acc[me] = part[me]
-    others = pl.ds(0, n - 1)
-    copies = remote(part.at[others], acc.at[others], send, recv, lax.rem(me + 1, n))
-    copies.wait_recv()
-    y_own = functools.reduce(jnp.add, [acc[p] for p in range(n)]).astype(jnp.bfloat16)
-    out[...] = (h2[...].astype(f32) + y_own.astype(f32) * gate[:, 0:1]).astype(jnp.bfloat16)
-    copies.wait_send()
+    _, _, _, _, (diag, diag_o, x_same, y_same, x_o, y_o, pair) = neighbours(me)
+    to_pair = [remote(part.at[d], near.at[t], s1.at[t], r1.at[t], pair) for t, d in enumerate((diag, x_same, y_same, pair))]
+    for c in to_pair:
+        c.start()
+    to_far = []
+    for t, d in enumerate((diag_o, x_o, y_o)):
+        to_pair[t].wait_recv()
+        mixed[t] = part[d] + near[t]
+        to_far.append(remote(mixed.at[t], far.at[t], s2.at[t], r2.at[t], d))
+        to_far[-1].start()
+    to_pair[3].wait_recv()
+    y_own = part[me] + near[3]
+    for t, c in enumerate(to_far):
+        c.wait_recv()
+        y_own = y_own + far[t]
+    out[...] = (h2[...].astype(f32) + y_own.astype(jnp.bfloat16).astype(f32) * gate[:, 0:1]).astype(jnp.bfloat16)
+    for c in to_pair + to_far:
+        c.wait_send()
 
 
 def solution(mesh):
@@ -483,7 +492,8 @@
             out_shape=jax.ShapeDtypeStruct((rows, width), bf16),
             in_specs=[VMEM] * 3,
             out_specs=VMEM,
-            scratch_shapes=[pltpu.VMEM((n, rows, width), f32), dma, dma],
+            scratch_shapes=[pltpu.VMEM((4, rows, width), f32), pltpu.VMEM((3, rows, width), f32),
+                            pltpu.VMEM((3, rows, width), f32), dma((4,)), dma((4,)), dma((3,)), dma((3,))],
             compiler_params=pltpu.CompilerParams(collective_id=1, has_side_effects=True, vmem_limit_bytes=4 << 20),
             name='experts')(part, gate, h2)
 

time: 48.5 us -> 47.9 us (0.988)
  Pallas kernels: 47.1 us -> 46.4 us
    pallas_call x1, Pallas kernels: 7.35 us -> 6.7 us  [decoder_block(): pl.pallas_call(functools.partial(reduce_kernel, n), out_shape=jax.ShapeDt...]
where the time goes in v6:
time: 47.9 us; the launch traced here: 47.8 us
  Pallas kernels  46.4 us (97%)
  between operations  0.71 us (1%)
  local copies, waits for them, and re-layouts  0.62 us (1%)
    pallas_call x1, Pallas kernels, decoder_block(): pl.pallas_call(functools.partial(gather_kernel, n, head_dim), out_shape=(...  30.8 us
    pallas_call x1, Pallas kernels, decoder_block(): pl.pallas_call(functools.partial(update_kernel, n, capacity), out_shape=(...  8.91 us
    pallas_call x1, Pallas kernels, decoder_block(): pl.pallas_call(functools.partial(reduce_kernel, n), out_shape=jax.ShapeDt...  6.7 us

profile of v6, /device:TPU:0, one launch (start us, length us, event | category | flops | bytes accessed | tf_op | source)
XLA Modules:
  0.0 47.8 jit_solution(1362289303772963742)
XLA Ops:
  0.6 0.0 copy-start
  0.6 0.0 copy-start.1
  0.7 0.0 copy-start.2
  0.7 30.8 %gather.1 = (bf16[16,768]{1,0:T(8,128)(2,1)S(1)}, bf16[8,16,768]{2,1,0:T(8,128)(2,1)S(1)}, s32[8,16,128]{2,1,0:T(8,128)S(1)}, f32[8,1,768]{2,1,0:T(1,128)S(1)}, ...) custom-call(bf16[16,768]{1,0:T(8,128)(2,1)} %hid.1, ...), custom_call_target="tpu_custom_call" | custom-call | tf_op jit(solution)/shard_map/gather/pallas_call | solution.py:460
  31.5 0.0 copy-done
  31.5 0.0 copy-done.1
  31.5 0.0 copy-done.2
  31.5 8.9 %attend.1 = (f32[8,16,768]{2,1,0:T(8,128)S(1)}, f32[16,128]{1,0:T(8,128)S(1)}, bf16[16,768,512]{2,1,0:T(8,128)(2,1)}, bf16[16,768,512]{2,1,0:T(8,128)(2,1)}, bf1...) custom-call(s32[16]{0:T(128)S(1)} %copy-done.2, ...), custom_call_target="tpu_custom_call", output_to_operand_aliasing={{4}: (8, {}), {5}: (9, {}), {6}: (10, {}), {7}: (11, {})} | custom-call | tf_op jit(solution)/shard_map/attend/pallas_call | solution.py:479
  40.4 6.7 %experts.1 = bf16[16,768]{1,0:T(8,128)(2,1)S(1)} custom-call(f32[8,16,768]{2,1,0:T(8,128)S(1)} %get-tuple-element.26.part, f32[16,128]{1,0:T(8,128)S(1)} %get-tuple-element.27.gate, bf16[16,768]{1,0:T(8,128)(2,1)S(1)} %get-tuple-element.28.h2), custom_call_target="tpu_custom_call" | custom-call | tf_op jit(solution)/shard_map/experts/pallas_call | solution.py:490
  47.2 0.6 %copy.33 = bf16[16,768]{1,0:T(8,128)(2,1)} copy(bf16[16,768]{1,0:T(8,128)(2,1)S(1)} %experts.1) | data formatting | bytes 49152
Async XLA Ops:
  0.6 30.9 %copy-start = (bf16[8,768,384]{2,1,0:T(8,128)(2,1)S(1)}, bf16[8,768,384]{2,1,0:T(8,128)(2,1)}, u32[]{:S(2)}) copy-start(bf16[8,768,384]{2,1,0:T(8,128)(2,1)} %win.1) | copy-start | bytes 14155780
  0.6 30.9 %copy-start.1 = (bf16[8,384,768]{2,1,0:T(8,128)(2,1)S(1)}, bf16[8,384,768]{2,1,0:T(8,128)(2,1)}, u32[]{:S(2)}) copy-start(bf16[8,384,768]{2,1,0:T(8,128)(2,1)} %wout.1) | copy-start | bytes 14155780
  0.7 30.9 %copy-start.2 = (s32[16]{0:T(128)S(1)}, s32[16]{0:T(128)}, u32[]{:S(2)}) copy-start(s32[16]{0:T(128)} %pos.3) | copy-start | bytes 196

commit v7 on v6

--- a/solution.py
+++ b/solution.py
@@ -299,8 +299,8 @@
     over_rows(piece, rows, cross_scores)
     relay_rest(2)
     over_rows(0, rows, cross_softmax, SOFTMAX_GROUP)
+    over_rows(0, piece, cross_context)
     relay_diag(2)
-    over_rows(0, piece, cross_context)
     load_late.wait()
     over_rows(piece, rows, cross_context_late)
     wait_weight(2)

time: 47.9 us -> 47.5 us (level)
    pallas_call x1, Pallas kernels: 6.7 us -> 6.19 us  [decoder_block(): pl.pallas_call(functools.partial(reduce_kernel, n), out_shape=jax.ShapeDt...]
where the time goes in v7:
time: 47.5 us; the launch traced here: 47.4 us
  Pallas kernels  46 us (97%)
  between operations  0.71 us (1%)
  local copies, waits for them, and re-layouts  0.62 us (1%)
    pallas_call x1, Pallas kernels, decoder_block(): pl.pallas_call(functools.partial(gather_kernel, n, head_dim), out_shape=(...  30.9 us
    pallas_call x1, Pallas kernels, decoder_block(): pl.pallas_call(functools.partial(update_kernel, n, capacity), out_shape=(...  8.91 us
    pallas_call x1, Pallas kernels, decoder_block(): pl.pallas_call(functools.partial(reduce_kernel, n), out_shape=jax.ShapeDt...  6.19 us

profile of v7, /device:TPU:0, one launch (start us, length us, event | category | flops | bytes accessed | tf_op | source)
XLA Modules:
  0.0 47.4 jit_solution(1772561086245479750)
XLA Ops:
  0.6 0.0 copy-start
  0.6 0.0 copy-start.1
  0.7 0.0 copy-start.2
  0.7 30.9 %gather.1 = (bf16[16,768]{1,0:T(8,128)(2,1)S(1)}, bf16[8,16,768]{2,1,0:T(8,128)(2,1)S(1)}, s32[8,16,128]{2,1,0:T(8,128)S(1)}, f32[8,1,768]{2,1,0:T(1,128)S(1)}, ...) custom-call(bf16[16,768]{1,0:T(8,128)(2,1)} %hid.1, ...), custom_call_target="tpu_custom_call" | custom-call | tf_op jit(solution)/shard_map/gather/pallas_call | solution.py:460
  31.6 0.0 copy-done
  31.6 0.0 copy-done.1
  31.6 0.0 copy-done.2
  31.6 8.9 %attend.1 = (f32[8,16,768]{2,1,0:T(8,128)S(1)}, f32[16,128]{1,0:T(8,128)S(1)}, bf16[16,768,512]{2,1,0:T(8,128)(2,1)}, bf16[16,768,512]{2,1,0:T(8,128)(2,1)}, bf1...) custom-call(s32[16]{0:T(128)S(1)} %copy-done.2, ...), custom_call_target="tpu_custom_call", output_to_operand_aliasing={{4}: (8, {}), {5}: (9, {}), {6}: (10, {}), {7}: (11, {})} | custom-call | tf_op jit(solution)/shard_map/attend/pallas_call | solution.py:479
  40.6 6.2 %experts.1 = bf16[16,768]{1,0:T(8,128)(2,1)S(1)} custom-call(f32[8,16,768]{2,1,0:T(8,128)S(1)} %get-tuple-element.26.part, f32[16,128]{1,0:T(8,128)S(1)} %get-tuple-element.27.gate, bf16[16,768]{1,0:T(8,128)(2,1)S(1)} %get-tuple-element.28.h2), custom_call_target="tpu_custom_call" | custom-call | tf_op jit(solution)/shard_map/experts/pallas_call | solution.py:490
  46.8 0.6 %copy.33 = bf16[16,768]{1,0:T(8,128)(2,1)} copy(bf16[16,768]{1,0:T(8,128)(2,1)S(1)} %experts.1) | data formatting | bytes 49152
Async XLA Ops:
  0.6 31.0 %copy-start = (bf16[8,768,384]{2,1,0:T(8,128)(2,1)S(1)}, bf16[8,768,384]{2,1,0:T(8,128)(2,1)}, u32[]{:S(2)}) copy-start(bf16[8,768,384]{2,1,0:T(8,128)(2,1)} %win.1) | copy-start | bytes 14155780
  0.6 31.0 %copy-start.1 = (bf16[8,384,768]{2,1,0:T(8,128)(2,1)S(1)}, bf16[8,384,768]{2,1,0:T(8,128)(2,1)}, u32[]{:S(2)}) copy-start(bf16[8,384,768]{2,1,0:T(8,128)(2,1)} %wout.1) | copy-start | bytes 14155780
  0.7 31.0 %copy-start.2 = (s32[16]{0:T(128)S(1)}, s32[16]{0:T(128)}, u32[]{:S(2)}) copy-start(s32[16]{0:T(128)} %pos.3) | copy-start | bytes 196

commit v8 on v7

--- a/solution.py
+++ b/solution.py
@@ -271,9 +271,6 @@
     wait_weight(0)
     h1 = (hid_v[...].astype(f32) + project(contexts(), wo_all[...])).astype(bf16)
     relay(2)
-    for p in peers:
-        remote(eid_all.at[me], eid_all.at[me], send.at[1], recv.at[1], p).start()
-        remote(wr_all.at[me], wr_all.at[me], send.at[2], recv.at[2], p).start()
 
     wait_weight(1)
     q_sc[...] = project(rms_norm(h1, ln_cv[...]), wqc_all[...]).astype(bf16).astype(f32)
@@ -298,6 +295,9 @@
     load_late = local(cv.at[pl.ds(piece, piece)], ck_v.at[pl.ds(0, piece)])
     over_rows(piece, rows, cross_scores)
     relay_rest(2)
+    for p in peers:
+        remote(eid_all.at[me], eid_all.at[me], send.at[1], recv.at[1], p).start()
+        remote(wr_all.at[me], wr_all.at[me], send.at[2], recv.at[2], p).start()
     over_rows(0, rows, cross_softmax, SOFTMAX_GROUP)
     over_rows(0, piece, cross_context)
     relay_diag(2)

time: 47.5 us -> 47.5 us (level)
  no operation moved by 1% of the time
where the time goes in v8:
time: 47.5 us; the launch traced here: 47.3 us
  Pallas kernels  46 us (97%)
  between operations  0.71 us (1%)
  local copies, waits for them, and re-layouts  0.62 us (1%)
    pallas_call x1, Pallas kernels, decoder_block(): pl.pallas_call(functools.partial(gather_kernel, n, head_dim), out_shape=(...  30.9 us
    pallas_call x1, Pallas kernels, decoder_block(): pl.pallas_call(functools.partial(update_kernel, n, capacity), out_shape=(...  8.91 us
    pallas_call x1, Pallas kernels, decoder_block(): pl.pallas_call(functools.partial(reduce_kernel, n), out_shape=jax.ShapeDt...  6.17 us

profile of v8, /device:TPU:0, one launch (start us, length us, event | category | flops | bytes accessed | tf_op | source)
XLA Modules:
  0.0 47.3 jit_solution(11443870929736599311)
XLA Ops:
  0.6 0.0 copy-start
  0.6 0.0 copy-start.1
  0.7 0.0 copy-start.2
  0.7 30.9 %gather.1 = (bf16[16,768]{1,0:T(8,128)(2,1)S(1)}, bf16[8,16,768]{2,1,0:T(8,128)(2,1)S(1)}, s32[8,16,128]{2,1,0:T(8,128)S(1)}, f32[8,1,768]{2,1,0:T(1,128)S(1)}, ...) custom-call(bf16[16,768]{1,0:T(8,128)(2,1)} %hid.1, ...), custom_call_target="tpu_custom_call" | custom-call | tf_op jit(solution)/shard_map/gather/pallas_call | solution.py:460
  31.6 0.0 copy-done
  31.6 0.0 copy-done.1
  31.6 0.0 copy-done.2
  31.6 8.9 %attend.1 = (f32[8,16,768]{2,1,0:T(8,128)S(1)}, f32[16,128]{1,0:T(8,128)S(1)}, bf16[16,768,512]{2,1,0:T(8,128)(2,1)}, bf16[16,768,512]{2,1,0:T(8,128)(2,1)}, bf1...) custom-call(s32[16]{0:T(128)S(1)} %copy-done.2, ...), custom_call_target="tpu_custom_call", output_to_operand_aliasing={{4}: (8, {}), {5}: (9, {}), {6}: (10, {}), {7}: (11, {})} | custom-call | tf_op jit(solution)/shard_map/attend/pallas_call | solution.py:479
  40.6 6.2 %experts.1 = bf16[16,768]{1,0:T(8,128)(2,1)S(1)} custom-call(f32[8,16,768]{2,1,0:T(8,128)S(1)} %get-tuple-element.26.part, f32[16,128]{1,0:T(8,128)S(1)} %get-tuple-element.27.gate, bf16[16,768]{1,0:T(8,128)(2,1)S(1)} %get-tuple-element.28.h2), custom_call_target="tpu_custom_call" | custom-call | tf_op jit(solution)/shard_map/experts/pallas_call | solution.py:490
  46.7 0.6 %copy.33 = bf16[16,768]{1,0:T(8,128)(2,1)} copy(bf16[16,768]{1,0:T(8,128)(2,1)S(1)} %experts.1) | data formatting | bytes 49152
Async XLA Ops:
  0.6 31.0 %copy-start = (bf16[8,768,384]{2,1,0:T(8,128)(2,1)S(1)}, bf16[8,768,384]{2,1,0:T(8,128)(2,1)}, u32[]{:S(2)}) copy-start(bf16[8,768,384]{2,1,0:T(8,128)(2,1)} %win.1) | copy-start | bytes 14155780
  0.6 31.0 %copy-start.1 = (bf16[8,384,768]{2,1,0:T(8,128)(2,1)S(1)}, bf16[8,384,768]{2,1,0:T(8,128)(2,1)}, u32[]{:S(2)}) copy-start(bf16[8,384,768]{2,1,0:T(8,128)(2,1)} %wout.1) | copy-start | bytes 14155780
  0.7 31.0 %copy-start.2 = (s32[16]{0:T(128)S(1)}, s32[16]{0:T(128)}, u32[]{:S(2)}) copy-start(s32[16]{0:T(128)} %pos.3) | copy-start | bytes 196
